TPU v7x, 256 devices: a whole 4x4x8 slice. The times are simulated.
256 devices in a mesh: rows: 16 (over x, y_hi, core), mp: 16 (over y_lo, z).
Axes of the slice: x: 4, y: 4 (y_hi: 2, y_lo: 2; y = y_hi * 2 + y_lo), z: 8, core: 2. Of those that a mesh axis runs over, the one named last changes fastest.
Arguments:
- tokens: bfloat16 [2048, 3584], P('rows', 'mp'), may hold values from -6 to 6
- modality: int32 [2048], replicated, may hold values from 0 to 1, as said below
- attn_gain: float32 [2, 3584], P(None, 'mp'), may hold values from 0.1 to 1.9
- ffn_gain: float32 [2, 3584], P(None, 'mp'), may hold values from 0.1 to 1.9
- w_query: bfloat16 [2, 3584, 2048], P(None, 'mp', 'rows'), may hold values from -4 to 4
- w_keyval: bfloat16 [2, 3584, 1024], P(None, 'mp', 'rows'), may hold values from -4 to 4
- w_out: bfloat16 [2, 2048, 3584], P(None, 'rows', 'mp'), may hold values from -0.125 to 0.125
- w_gate: bfloat16 [2, 3584, 9472], P(None, 'mp', 'rows'), may hold values from -0.09375 to 0.09375
- w_up: bfloat16 [2, 3584, 9472], P(None, 'mp', 'rows'), may hold values from -0.09375 to 0.09375
- w_down: bfloat16 [2, 9472, 3584], P(None, 'rows', 'mp'), may hold values from -0.0625 to 0.0625
Outputs:
- mixed: bfloat16 [2048, 3584], P('rows', 'mp')
Inputs may be any that keep to these rules, and one draw needn't show every extreme that they name: `modality`: constant over each aligned block of 128 positions.
All inputs are finite; a program needn't handle non-finite values.
Results may differ from a plain program's by a relative error of at most 0.024.
Values may be sent and summed in bfloat16 or wider, within the bound.
A program may use at most 64 MiB of HBM per device.

v0:
```python
import jax
import jax.numpy as jnp
from jax import lax
from jax.sharding import Mesh
from jax.sharding import PartitionSpec as P

D = 3584
HD = 128
KV = 4
HEADS = 16
MODAL_BLOCK = 128
MP = ("mp_0", "mp_1")


EPSILON = 1e-06


def from_everyone(value, axis):
    copies = jnp.broadcast_to(value, (lax.axis_size(axis), *value.shape))
    return lax.all_to_all(copies, axis, split_axis=0, concat_axis=0, tiled=True)


def over_copies(value, axis):
    everything = from_everyone(value, axis)
    return jnp.sum(everything, axis=0)


def laid_out(blocks, dim):
    shape = list(blocks.shape[1:])
    shape[dim] *= blocks.shape[0]
    return jnp.moveaxis(blocks, 0, dim).reshape(shape)


def gather_directly(value, axis, dim):
    return laid_out(from_everyone(value, axis), dim)


def cut_along(value, dim, peers):
    shape = value.shape
    blocks = value.reshape(*shape[:dim], peers, shape[dim] // peers, *shape[dim + 1 :])
    return jnp.moveaxis(blocks, dim, 0)


def sent_and_summed(value, axis, dim):
    blocks = cut_along(value, dim, lax.axis_size(axis))
    arrived = lax.all_to_all(blocks, axis, split_axis=0, concat_axis=0, tiled=True)
    return arrived.astype(jnp.float32).sum(axis=0)


def reduced_to_own(blocks, axes, sequence):
    inside = blocks.shape[1:]
    blocks = blocks.reshape(*(lax.axis_size(a) for a in axes), *inside)
    blocks = jnp.moveaxis(blocks, sequence, range(len(axes))).reshape(-1, *inside)
    for k in sequence:
        blocks = lax.psum_scatter(blocks, axes[k], scatter_dimension=0, tiled=True)
    return blocks[0]


def summed_rows_2(value, axes, sequence, dim):
    peers = lax.axis_size(axes)
    return reduced_to_own(cut_along(value, dim, peers), axes, sequence)


def tower_rows(matrix, weights, tower_ids):
    per_block = matrix.shape[0] // tower_ids.shape[0]
    token_towers = jnp.repeat(tower_ids, per_block)
    is_image = (token_towers == 1)[:, None]
    nothing = jnp.zeros((), matrix.dtype)
    text_rows = jnp.where(is_image, nothing, matrix)
    image_rows = jnp.where(is_image, matrix, nothing)
    text_part = jnp.dot(text_rows, weights[0], preferred_element_type=jnp.float32)
    image_part = jnp.dot(image_rows, weights[1], preferred_element_type=jnp.float32)
    return text_part + image_part


def block_towers(modality):
    return modality.reshape(-1, MODAL_BLOCK)[:, 0]


def scaled_rows(hidden, squares, gains, token_towers):
    inverse = lax.rsqrt(squares / D + EPSILON)
    chosen = jnp.where(token_towers[:, None] == 1, gains[1][None, :], gains[0][None, :])
    return (hidden * inverse[:, None] * chosen).astype(jnp.bfloat16)


def pick_group(matrix, head_group):
    key_part = lax.dynamic_slice_in_dim(matrix, head_group * HD, HD, 1)
    value_part = lax.dynamic_slice_in_dim(matrix, KV * HD + head_group * HD, HD, 1)
    return jnp.concatenate((key_part, value_part), axis=1)


def local(tokens, modality, attn_gain, ffn_gain, w_query, w_keyval, w_out, w_gate, w_up, w_down):
    row_count = tokens.shape[0]
    total_rows = row_count * lax.axis_size("rows")
    share_rows = total_rows // lax.axis_size(MP)
    row_index = lax.axis_index("rows")
    mp_index = lax.axis_index(MP)
    own_towers = lax.dynamic_slice_in_dim(modality, row_index * row_count, row_count)
    hidden = tokens.astype(jnp.float32)
    squares = over_copies(jnp.sum(hidden * hidden, axis=1), MP)
    normed = scaled_rows(hidden, squares, attn_gain, own_towers)
    normed_all = gather_directly(normed, "rows", 0)
    joint_weight = jnp.concatenate((w_query, w_keyval), axis=2)
    picked = normed_all
    projected = sent_and_summed(
        tower_rows(picked, joint_weight, block_towers(modality)).astype(jnp.bfloat16), MP, 0
    ).astype(jnp.bfloat16)
    query_width = w_query.shape[2]
    heads_here = query_width // HD
    queries = projected[:, :query_width].reshape(share_rows, heads_here, HD)
    keyval_local = projected[:, query_width:]
    head_group = row_index * heads_here // (HEADS // KV)
    keyval_block = gather_directly(keyval_local, "rows", 1)
    keyval_all = gather_directly(pick_group(keyval_block, head_group), MP, 0)
    scores = jnp.einsum(
        "qhd,kd->hqk", queries, keyval_all[:, :HD], preferred_element_type=jnp.float32
    ) * HD ** (-0.5)
    query_pos = mp_index * share_rows + jnp.arange(share_rows, dtype=jnp.int32)
    key_pos = jnp.arange(total_rows, dtype=jnp.int32)
    allowed = key_pos[None, :] <= query_pos[:, None]
    scores = jnp.where(allowed[None, :, :], scores, -1e30)
    largest = jnp.max(scores, axis=2, keepdims=True)
    powers = jnp.exp(scores - largest)
    probs = (powers / jnp.sum(powers, axis=2, keepdims=True)).astype(jnp.bfloat16)
    context = jnp.einsum(
        "hqk,kd->qhd", probs, keyval_all[:, HD:], preferred_element_type=jnp.float32
    )
    context = context.astype(jnp.bfloat16).reshape(share_rows, query_width)
    context_all = gather_directly(context, MP, 0)
    picked = context_all
    residual = hidden + sent_and_summed(
        tower_rows(picked, w_out, block_towers(modality)).astype(jnp.bfloat16), "rows", 0
    )
    squares_ffn = over_copies(jnp.sum(residual * residual, axis=1), MP)
    normed_ffn = scaled_rows(residual, squares_ffn, ffn_gain, own_towers)
    normed_ffn_all = gather_directly(normed_ffn, "rows", 0)
    pair_weight = jnp.concatenate((w_gate, w_up), axis=2)
    hidden_width = w_gate.shape[2]
    picked = normed_ffn_all
    summed = summed_rows_2(
        tower_rows(picked, pair_weight, block_towers(modality)).astype(jnp.bfloat16), MP, (1, 0), 0
    ).astype(jnp.float32)
    activated = (jax.nn.silu(summed[:, :hidden_width]) * summed[:, hidden_width:]).astype(
        jnp.bfloat16
    )
    activated_all = lax.all_gather(activated, MP, axis=0, tiled=True)
    picked = activated_all
    mixed = residual + sent_and_summed(
        tower_rows(picked, w_down, block_towers(modality)).astype(jnp.bfloat16), "rows", 0
    )
    return mixed.astype(jnp.bfloat16)


def solution(mesh):
    torus = Mesh(mesh.devices.reshape(mesh.shape["rows"], 2, 8), ("rows", "mp_0", "mp_1"))
    in_specs = (
        P("rows", MP),
        P(),
        P(None, MP),
        P(None, MP),
        P(None, MP, "rows"),
        P(None, MP, "rows"),
        P(None, "rows", MP),
        P(None, MP, "rows"),
        P(None, MP, "rows"),
        P(None, "rows", MP),
    )
    out_specs = P("rows", MP)
    return jax.shard_map(local, mesh=torus, in_specs=in_specs, out_specs=out_specs, check_vma=False)
```

profile of v0, /device:TPU:4, one launch (start us, length us, event | category | flops | bytes accessed | tf_op | source)
XLA Modules:
  0.0 393.0 jit_solution(9332766273389813539)
XLA Ops:
  6.5 0.9 fusion.44
  7.4 0.6 broadcast_in_dim.161
  8.0 9.6 %all-to-all-start = ((f32[16,1,128]{2,1,0:T(1,128)}), f32[16,1,128]{2,1,0:T(1,128)S(1)}, u32[]{:S(2)}, u32[]{:S(2)}) async-start(f32[16,1,128]{2,1,0:T(1,128)} %broadcast_in_dim.161), calls=%async_computation | async-start | bytes 16384 | tf_op jit(solution)/shard_map/all_to_all | solution.py:20
  17.6 0.8 fusion.66
  18.4 0.8 dynamic-slice_compare_fusion
  19.2 6.9 %all-to-all-done = f32[16,1,128]{2,1,0:T(1,128)S(1)} async-done(((f32[16,1,128]{2,1,0:T(1,128)}), f32[16,1,128]{2,1,0:T(1,128)S(1)}, u32[]{:S(2)}, u32[]{:S(2)}) %all-to-all-start) | async-done | bytes 8224 | tf_op jit(solution)/shard_map/all_to_all | solution.py:20
  26.1 0.9 fusion.46
  27.0 1.1 broadcast_in_dim.167
  28.1 7.2 %all-to-all-start.1 = ((bf16[16,128,224]{1,2,0:T(8,128)(2,1)}), bf16[16,128,224]{1,2,0:T(8,128)(2,1)S(1)}, u32[]{:S(2)}, u32[]{:S(2)}) async-start(bf16[16,128,224]{1,2,0:T(8,128)(2,1)} %broadcast_in_dim.167), calls=%async_computation.1 | async-start | bytes 1835008 | tf_op jit(solution)/shard_map/all_to_all | solution.py:20
  35.5 14.0 %all-to-all-done.1 = bf16[16,128,224]{1,2,0:T(8,128)(2,1)S(1)} async-done(((bf16[16,128,224]{1,2,0:T(8,128)(2,1)}), bf16[16,128,224]{1,2,0:T(8,128)(2,1)S(1)}, u32[]{:S(2)}, u32[]{:S(2)}) %all-to-all-start.1) | async-done | bytes 917536 | tf_op jit(solution)/shard_map/all_to_all | solution.py:20
  49.5 0.2 select_bitcast_fusion.2
  49.7 0.4 fusion.27
  50.1 0.4 fusion.15
  50.5 0.2 copy.98
  50.7 24.0 %all_to_all.52 = bf16[16,128,192]{1,2,0:T(8,128)(2,1)S(1)} all-to-all(bf16[16,128,192]{1,2,0:T(8,128)(2,1)S(1)} %bitcast.107), channel_id=1, replica_groups=mesh['rows'=16,'mp_0'=2,'mp_1'=8] {'mp_0','mp_1'}, dimensions={0} | all-to-all | bytes 1572864 | tf_op jit(solution)/shard_map/all_to_all | solution.py:46
  74.8 0.7 broadcast_in_dim.168
  75.6 5.9 %all-to-all-start.3 = ((bf16[16,128,64]{1,2,0:T(8,128)(2,1)}), bf16[16,128,64]{1,2,0:T(8,128)(2,1)S(1)}, u32[]{:S(2)}, u32[]{:S(2)}) async-start(bf16[16,128,64]{1,2,0:T(8,128)(2,1)} %broadcast_in_dim.168), calls=%async_computation.3 | async-start | bytes 524288 | tf_op jit(solution)/shard_map/all_to_all | solution.py:20
  81.5 6.9 %all-to-all-done.3 = bf16[16,128,64]{1,2,0:T(8,128)(2,1)S(1)} async-done(((bf16[16,128,64]{1,2,0:T(8,128)(2,1)}), bf16[16,128,64]{1,2,0:T(8,128)(2,1)S(1)}, u32[]{:S(2)}, u32[]{:S(2)}) %all-to-all-start.3) | async-done | bytes 262176 | tf_op jit(solution)/shard_map/all_to_all | solution.py:20
  88.5 1.1 broadcast_in_dim.169
  89.6 4.4 %all-to-all-start.4 = ((bf16[16,128,256]{2,1,0:T(8,128)(2,1)}), bf16[16,128,256]{2,1,0:T(8,128)(2,1)S(1)}, u32[]{:S(2)}, u32[]{:S(2)}) async-start(bf16[16,128,256]{2,1,0:T(8,128)(2,1)} %broadcast_in_dim.169), calls=%async_computation.4 | async-start | bytes 2097152 | tf_op jit(solution)/shard_map/all_to_all | solution.py:20
  94.1 27.5 %all-to-all-done.4 = bf16[16,128,256]{2,1,0:T(8,128)(2,1)S(1)} async-done(((bf16[16,128,256]{2,1,0:T(8,128)(2,1)}), bf16[16,128,256]{2,1,0:T(8,128)(2,1)S(1)}, u32[]{:S(2)}, u32[]{:S(2)}) %all-to-all-start.4) | async-done | bytes 1048608 | tf_op jit(solution)/shard_map/all_to_all | solution.py:20
  121.6 0.4 fusion.68
  122.1 0.3 fusion.19
  122.3 0.4 fusion.18
  122.9 19.8 %all_to_all.53 = bf16[16,128,128]{2,1,0:T(8,128)(2,1)S(1)} all-to-all(bf16[16,128,128]{2,1,0:T(8,128)(2,1)S(1)} %broadcast_in_dim.171), channel_id=1, replica_groups=mesh['rows'=16,'mp_0'=2,'mp_1'=8] {'mp_0','mp_1'}, dimensions={0} | all-to-all | bytes 1048576 | tf_op jit(solution)/shard_map/all_to_all | solution.py:20
  142.9 0.4 fusion.54
  143.3 0.4 fusion.11
  143.9 19.1 %all_to_all.54 = bf16[16,128,224]{1,2,0:T(8,128)(2,1)S(1)} all-to-all(bf16[16,128,224]{1,2,0:T(8,128)(2,1)S(1)} %bitcast.105), channel_id=1, replica_groups=mesh['rows'=16,'mp_0'=2,'mp_1'=8] {'rows'}, dimensions={0} | all-to-all | bytes 1835008 | tf_op jit(solution)/shard_map/all_to_all | solution.py:46
  163.2 0.6 broadcast_in_dim.175
  163.8 4.4 %all-to-all-start.7 = ((f32[16,1,128]{2,1,0:T(1,128)}), f32[16,1,128]{2,1,0:T(1,128)S(1)}, u32[]{:S(2)}, u32[]{:S(2)}) async-start(f32[16,1,128]{2,1,0:T(1,128)} %broadcast_in_dim.175), calls=%async_computation.7 | async-start | bytes 16384 | tf_op jit(solution)/shard_map/all_to_all | solution.py:20
  168.3 8.3 %all-to-all-done.7 = f32[16,1,128]{2,1,0:T(1,128)S(1)} async-done(((f32[16,1,128]{2,1,0:T(1,128)}), f32[16,1,128]{2,1,0:T(1,128)S(1)}, u32[]{:S(2)}, u32[]{:S(2)}) %all-to-all-start.7) | async-done | bytes 8224 | tf_op jit(solution)/shard_map/all_to_all | solution.py:20
  177.0 19.4 %all_to_all.55 = bf16[16,128,224]{1,2,0:T(8,128)(2,1)S(1)} all-to-all(bf16[16,128,224]{1,2,0:T(8,128)(2,1)S(1)} %broadcast_in_dim.180), channel_id=1, replica_groups=mesh['rows'=16,'mp_0'=2,'mp_1'=8] {'rows'}, dimensions={0} | all-to-all | bytes 1835008 | tf_op jit(solution)/shard_map/all_to_all | solution.py:20
  196.3 0.2 select_bitcast_fusion
  196.5 0.9 copy-done
  197.4 0.2 copy-done.1
  197.6 1.7 fusion.22
  199.2 1.8 fusion.10
  201.0 1.6 copy.76
  202.6 3.4 copy.67
  206.1 55.5 %reduce-scatter.3.cloned.1.call-done = bf16[2,128,1184]{1,2,0:T(8,128)(2,1)} async-done(((bf16[16,128,1184]{1,2,0:T(8,128)(2,1)}), bf16[2,128,1184]{1,2,0:T(8,128)(2,1)}) %reduce-scatter.3.cloned.1.call-update) | async-done | bytes 606224 | tf_op jit(solution)/shard_map/reduce_scatter | solution.py:55
  261.7 21.7 %reduce-scatter.5.cloned.1.call-done = bf16[1,128,1184]{1,2,0:T(8,128)(2,1)} async-done(((bf16[2,128,1184]{1,2,0:T(8,128)(2,1)}), bf16[1,128,1184]{1,2,0:T(8,128)(2,1)}) %reduce-scatter.5.cloned.1.call-update) | async-done | bytes 303120 | tf_op jit(solution)/shard_map/reduce_scatter | solution.py:55
  283.5 1.0 bitcast_convert_fusion
  284.5 0.7 fusion.39
  285.3 75.6 %all-gather.2.cloned.1.call-done = bf16[2048,592]{0,1:T(8,128)(2,1)} async-done(((bf16[128,592]{0,1:T(8,128)(2,1)}), bf16[2048,592]{0,1:T(8,128)(2,1)}) %all-gather.2.cloned.1.call-update) | async-done | bytes 2424848 | tf_op jit(solution)/shard_map/all_gather | solution.py:146
  360.9 2.7 fusion.5
  363.6 0.9 fusion.12
  364.7 21.0 %all_to_all.56 = bf16[16,128,224]{1,2,0:T(8,128)(2,1)S(1)} all-to-all(bf16[16,128,224]{1,2,0:T(8,128)(2,1)S(1)} %bitcast.106), channel_id=1, replica_groups=mesh['rows'=16,'mp_0'=2,'mp_1'=8] {'rows'}, dimensions={0} | all-to-all | bytes 1835008 | tf_op jit(solution)/shard_map/all_to_all | solution.py:46
  385.9 0.7 add_convert_fusion.1
  (48 shorter events, 2.0 us)
Async XLA Ops:
  6.5 28.8 %copy-start.6 = (s32[2048]{0:T(1024)S(1)}, s32[2048]{0:T(1024)}, u32[]{:S(2)}) copy-start(s32[2048]{0:T(1024)} %param.11) | copy-start | bytes 24580
  6.5 28.7 %copy-start.5 = (bf16[2,224,64]{1,2,0:T(8,128)(2,1)S(1)}, bf16[2,224,64]{1,2,0:T(8,128)(2,1)}, u32[]{:S(2)}) copy-start(bf16[2,224,64]{1,2,0:T(8,128)(2,1)} %param.15) | copy-start | bytes 172036
  8.0 18.0 %all-to-all-start = ((f32[16,1,128]{2,1,0:T(1,128)}), f32[16,1,128]{2,1,0:T(1,128)S(1)}, u32[]{:S(2)}, u32[]{:S(2)}) async-start(f32[16,1,128]{2,1,0:T(1,128)} %broadcast_in_dim.161), calls=%async_computation | async-start | bytes 16384 | tf_op jit(solution)/shard_map/all_to_all | solution.py:20
  28.1 21.4 %all-to-all-start.1 = ((bf16[16,128,224]{1,2,0:T(8,128)(2,1)}), bf16[16,128,224]{1,2,0:T(8,128)(2,1)S(1)}, u32[]{:S(2)}, u32[]{:S(2)}) async-start(bf16[16,128,224]{1,2,0:T(8,128)(2,1)} %broadcast_in_dim.167), calls=%async_computation.1 | async-start | bytes 1835008 | tf_op jit(solution)/shard_map/all_to_all | solution.py:20
  35.2 14.4 %copy-start.3 = (bf16[2,224,128]{2,1,0:T(8,128)(2,1)S(1)}, bf16[2,224,128]{2,1,0:T(8,128)(2,1)}, u32[]{:S(2)}) copy-start(bf16[2,224,128]{2,1,0:T(8,128)(2,1)} %param.14) | copy-start | bytes 344068
  75.6 12.8 %all-to-all-start.3 = ((bf16[16,128,64]{1,2,0:T(8,128)(2,1)}), bf16[16,128,64]{1,2,0:T(8,128)(2,1)S(1)}, u32[]{:S(2)}, u32[]{:S(2)}) async-start(bf16[16,128,64]{1,2,0:T(8,128)(2,1)} %broadcast_in_dim.168), calls=%async_computation.3 | async-start | bytes 524288 | tf_op jit(solution)/shard_map/all_to_all | solution.py:20
  89.6 32.0 %all-to-all-start.4 = ((bf16[16,128,256]{2,1,0:T(8,128)(2,1)}), bf16[16,128,256]{2,1,0:T(8,128)(2,1)S(1)}, u32[]{:S(2)}, u32[]{:S(2)}) async-start(bf16[16,128,256]{2,1,0:T(8,128)(2,1)} %broadcast_in_dim.169), calls=%async_computation.4 | async-start | bytes 2097152 | tf_op jit(solution)/shard_map/all_to_all | solution.py:20
  122.7 20.2 %copy-start.4 = (bf16[2,128,224]{1,2,0:T(8,128)(2,1)S(1)}, bf16[2,128,224]{1,2,0:T(8,128)(2,1)}, u32[]{:S(2)}) copy-start(bf16[2,128,224]{1,2,0:T(8,128)(2,1)} %param.16) | copy-start | bytes 344068
  143.9 19.3 %copy-start.2 = (bf16[128,224]{0,1:T(8,128)(2,1)S(1)}, bf16[128,224]{0,1:T(8,128)(2,1)}, u32[]{:S(2)}) copy-start(bf16[128,224]{0,1:T(8,128)(2,1)} %param.10) | copy-start | bytes 172036
  143.9 24.4 %copy-start.7 = (f32[2,224]{1,0:T(2,128)S(1)}, f32[2,224]{1,0:T(2,128)}, u32[]{:S(2)}) copy-start(f32[2,224]{1,0:T(2,128)} %param.13) | copy-start | bytes 5380
  163.8 12.9 %all-to-all-start.7 = ((f32[16,1,128]{2,1,0:T(1,128)}), f32[16,1,128]{2,1,0:T(1,128)S(1)}, u32[]{:S(2)}, u32[]{:S(2)}) async-start(f32[16,1,128]{2,1,0:T(1,128)} %broadcast_in_dim.175), calls=%async_computation.7 | async-start | bytes 16384 | tf_op jit(solution)/shard_map/all_to_all | solution.py:20
  168.3 93.4 %reduce-scatter.3.cloned.1.call-start = ((), (), s32[]{:S(2)}) async-start(), calls=%async_computation.12 | async-start | bytes 5455872 | tf_op jit(solution)/shard_map/reduce_scatter | solution.py:55
  196.3 1.1 copy-start
  196.3 1.2 copy-start.1
  206.1 154.8 %copy-start.9 = (bf16[2,592,224]{1,2,0:T(8,128)(2,1)S(1)}, bf16[2,592,224]{1,2,0:T(8,128)(2,1)}, u32[]{:S(2)}) copy-start(bf16[2,592,224]{1,2,0:T(8,128)(2,1)} %param.19) | copy-start | bytes 1591300
  206.1 77.4 %reduce-scatter.5.cloned.1.call-start = ((), (), s32[]{:S(2)}) async-start(), calls=%async_computation.13 | async-start | bytes 909312 | tf_op jit(solution)/shard_map/reduce_scatter | solution.py:55
  261.7 99.2 %all-gather.2.cloned.1.call-start = ((), (), s32[]{:S(2)}) async-start(), calls=%async_computation.14 | async-start | bytes 2576384 | tf_op jit(solution)/shard_map/all_gather | solution.py:146
  360.9 2.7 copy-start.8
Sparse Core Ops, SparseCore 0:
  206.2 55.4 reduce-scatter.2
  264.2 19.2 reduce-scatter.4
  285.4 75.4 all-gather.1
where the time goes:
time: 397 us; the launch traced here: 393 us
  waiting for transfers between devices  217 us (55%)
  blocking collectives  103 us (26%)
  starting transfers between devices  31.6 us (8%)
  between operations  13.4 us (3%)
  local copies, waits for them, and re-layouts  12.1 us (3%)
  matrix products  9.48 us (2%)
  other arithmetic  6.53 us (2%)
    reduce_scatter x2, waiting for transfers between devices, reduced_to_own(): blocks = lax.psum_scatter(blocks, axes[k], scatter_dimension=0, tiled=True)  77.3 us
    all_gather x1, waiting for transfers between devices, local(): activated_all = lax.all_gather(activated, MP, axis=0, tiled=True)  75.6 us
    all_to_all x3, blocking collectives, sent_and_summed(): lax.all_to_all(blocks, axis, split_axis=0, concat_axis=0, tiled=True)  64.2 us
    all_to_all x5, waiting for transfers between devices, from_everyone(): return lax.all_to_all(copies, axis, split_axis=0, concat_axis=0, tiled=True)  63.7 us
    all_to_all x2, blocking collectives, from_everyone(): return lax.all_to_all(copies, axis, split_axis=0, concat_axis=0, tiled=True)  39.1 us
    all_to_all x5, starting transfers between devices, from_everyone(): return lax.all_to_all(copies, axis, split_axis=0, concat_axis=0, tiled=True)  31.5 us
  transfers between devices with their start and end apart: 8, of which 8 were waited for; matrix products, arithmetic and copies ran while one was open for 0% of the time, Pallas kernels for 0%

commit v1 on v0

v1 whole, which is shorter than its diff:
```python
import functools

import jax
import jax.numpy as jnp
from jax import lax
from jax.experimental import pallas as pl
from jax.experimental.pallas import tpu as pltpu
from jax.sharding import Mesh
from jax.sharding import PartitionSpec as P

D = 3584
HD = 128
KV = 4
HEADS = 16
MODAL_BLOCK = 128
ROWS = ("x", "yh", "c")
MP = ("yl", "z")
AXES = ("x", "yh", "c", "yl", "z")
NX, NYH, NZ = 4, 2, 8
NB = NX * NYH

EPSILON = 1e-06
F32 = jnp.float32
BF16 = jnp.bfloat16


def from_everyone(value, axis):
    copies = jnp.broadcast_to(value, (lax.axis_size(axis), *value.shape))
    return lax.all_to_all(copies, axis, split_axis=0, concat_axis=0, tiled=True)


def over_copies(value, axis):
    everything = from_everyone(value, axis)
    return jnp.sum(everything, axis=0)


def laid_out(blocks, dim):
    shape = list(blocks.shape[1:])
    shape[dim] *= blocks.shape[0]
    return jnp.moveaxis(blocks, 0, dim).reshape(shape)


def gather_directly(value, axis, dim):
    return laid_out(from_everyone(value, axis), dim)


def cut_along(value, dim, peers):
    shape = value.shape
    blocks = value.reshape(*shape[:dim], peers, shape[dim] // peers, *shape[dim + 1 :])
    return jnp.moveaxis(blocks, dim, 0)


def sent_and_summed(value, axis, dim):
    blocks = cut_along(value, dim, lax.axis_size(axis))
    arrived = lax.all_to_all(blocks, axis, split_axis=0, concat_axis=0, tiled=True)
    return arrived.astype(jnp.float32).sum(axis=0)


def tower_rows(matrix, weights, tower_ids):
    per_block = matrix.shape[0] // tower_ids.shape[0]
    token_towers = jnp.repeat(tower_ids, per_block)
    is_image = (token_towers == 1)[:, None]
    nothing = jnp.zeros((), matrix.dtype)
    text_rows = jnp.where(is_image, nothing, matrix)
    image_rows = jnp.where(is_image, matrix, nothing)
    text_part = jnp.dot(text_rows, weights[0], preferred_element_type=jnp.float32)
    image_part = jnp.dot(image_rows, weights[1], preferred_element_type=jnp.float32)
    return text_part + image_part


def block_towers(modality):
    return modality.reshape(-1, MODAL_BLOCK)[:, 0]


def scaled_rows(hidden, squares, gains, token_towers):
    inverse = lax.rsqrt(squares / D + EPSILON)
    chosen = jnp.where(token_towers[:, None] == 1, gains[1][None, :], gains[0][None, :])
    return (hidden * inverse[:, None] * chosen).astype(jnp.bfloat16)


def pick_group(matrix, head_group):
    key_part = lax.dynamic_slice_in_dim(matrix, head_group * HD, HD, 1)
    value_part = lax.dynamic_slice_in_dim(matrix, KV * HD + head_group * HD, HD, 1)
    return jnp.concatenate((key_part, value_part), axis=1)


class Place:
    def __init__(self):
        self.at = {a: lax.axis_index(a) for a in AXES}
        self.x, self.h, self.c, self.l, self.z = (self.at[a] for a in AXES)
        self.same = 1 - (self.c - self.l) * (self.c - self.l)

    def id(self, **moved):
        return tuple(moved.get(a, self.at[a]) for a in AXES)

    def cross(self, dx, dh):
        return self.id(
            x=lax.rem(self.x + dx, NX), yh=lax.rem(self.h + dh, NYH), c=self.l, yl=self.c
        )

    def ahead(self, dx, dh):
        return NYH * lax.rem(self.x + dx, NX) + lax.rem(self.h + dh, NYH)

    def behind(self, dx, dh):
        return NYH * lax.rem(self.x - dx + NX, NX) + lax.rem(self.h - dh + NYH, NYH)

    def partner(self):
        return self.id(c=1 - self.c)

    def along(self, k):
        return lax.rem(self.z + k + NZ, NZ)


OFFSETS = tuple((dx, dh) for dx in (2, 1, 3, 0) for dh in (1, 0))


def sent(src, dst, send, recv, target):
    return pltpu.make_async_remote_copy(
        src_ref=src,
        dst_ref=dst,
        send_sem=send,
        recv_sem=recv,
        device_id=target,
        device_id_type=pl.DeviceIdType.MESH,
    )


def greet(place, peers):
    barrier = pltpu.get_barrier_semaphore()
    for peer in peers:
        pl.semaphore_signal(barrier, 1, device_id=peer, device_id_type=pl.DeviceIdType.MESH)
    count = len(peers)
    for dx, dh in OFFSETS:
        if (dx, dh) != (0, 0):
            pl.semaphore_signal(
                barrier, 1, device_id=place.cross(dx, dh), device_id_type=pl.DeviceIdType.MESH
            )
            count += 1

    @pl.when(place.c != place.l)
    def _():
        pl.semaphore_signal(
            barrier, 1, device_id=place.cross(0, 0), device_id_type=pl.DeviceIdType.MESH
        )

    pl.semaphore_wait(barrier, count + 1 - place.same)


def gather_rows(place, src, xg, sems):
    send, recv, fsend, frecv = (sems.at[k] for k in range(4))
    own = NYH * place.x + place.h
    for i, (dx, dh) in enumerate(OFFSETS):
        copy = sent(src, xg.at[place.l, own], send.at[i], recv.at[i], place.cross(dx, dh))
        if (dx, dh) != (0, 0):
            copy.start()
        else:
            pl.when(place.c != place.l)(copy.start)

            @pl.when(place.c == place.l)
            def _():
                xg[place.l, own] = src[...]

    order = sorted(range(NB), key=lambda i: (min(OFFSETS[i][0], NX - OFFSETS[i][0]), OFFSETS[i][1]))
    for i in order:
        dx, dh = OFFSETS[i]
        slot = xg.at[place.c, place.behind(dx, dh)]
        arrive = sent(slot, slot, send.at[i], recv.at[i], place.cross(dx, dh))
        if (dx, dh) != (0, 0):
            arrive.wait_recv()
        else:
            pl.when(place.c != place.l)(arrive.wait_recv)
        sent(slot, slot, fsend.at[i], frecv.at[i], place.partner()).start()
    for i in order:
        dx, dh = OFFSETS[i]
        slot = xg.at[1 - place.c, place.behind(dx, dh)]
        sent(slot, slot, fsend.at[i], frecv.at[i], place.partner()).wait_recv()


def gather_rows_end(place, src, xg, sems):
    send, recv, fsend, frecv = (sems.at[k] for k in range(4))
    for i, (dx, dh) in enumerate(OFFSETS):
        copy = sent(src, src, send.at[i], recv.at[i], place.cross(dx, dh))
        if (dx, dh) != (0, 0):
            copy.wait_send()
        else:
            pl.when(place.c != place.l)(copy.wait_send)
        slot = xg.at[place.c, place.behind(dx, dh)]
        sent(slot, slot, fsend.at[i], frecv.at[i], place.partner()).wait_send()


def reduce_rows(place, part, dbuf, rbuf, sems):
    send, recv, fsend, frecv = (sems.at[k] for k in range(4))
    own = NYH * place.x + place.h
    for i, (dx, dh) in enumerate(OFFSETS):
        j = place.ahead(dx, dh)
        sent(
            part.at[1 - place.c, j], dbuf.at[j], fsend.at[i], frecv.at[i], place.partner()
        ).start()
    for i, (dx, dh) in enumerate(OFFSETS):
        j = place.ahead(dx, dh)
        sent(part.at[1 - place.c, j], dbuf.at[j], fsend.at[i], frecv.at[i], place.partner()).wait_recv()
        total = part[place.c, j].astype(F32) + dbuf[j].astype(F32)
        dbuf[j] = total.astype(BF16)
        copy = sent(dbuf.at[j], rbuf.at[i], send.at[i], recv.at[i], place.cross(dx, dh))
        if (dx, dh) != (0, 0):
            copy.start()
        else:
            pl.when(place.c != place.l)(copy.start)

            @pl.when(place.c == place.l)
            def _():
                rbuf[i] = dbuf[own]

    total = None
    order = sorted(range(NB), key=lambda i: (min(OFFSETS[i][0], NX - OFFSETS[i][0]), OFFSETS[i][1]))
    for i in order:
        dx, dh = OFFSETS[i]
        arrive = sent(rbuf.at[i], rbuf.at[i], send.at[i], recv.at[i], place.cross(dx, dh))
        if (dx, dh) != (0, 0):
            arrive.wait_recv()
        else:
            pl.when(place.c != place.l)(arrive.wait_recv)
        term = rbuf[i].astype(F32)
        total = term if total is None else total + term
    for i, (dx, dh) in enumerate(OFFSETS):
        j = place.ahead(dx, dh)
        sent(part.at[1 - place.c, j], dbuf.at[j], fsend.at[i], frecv.at[i], place.partner()).wait_send()
        copy = sent(dbuf.at[j], rbuf.at[i], send.at[i], recv.at[i], place.cross(dx, dh))
        if (dx, dh) != (0, 0):
            copy.wait_send()
        else:
            pl.when(place.c != place.l)(copy.wait_send)
    return total


PARTS = 4


def sum_along_z(place, partial, pbuf, chain, sems):
    part_rows = MODAL_BLOCK // PARTS
    sides = (1, -1)

    def rows(q):
        return pl.ds(q * part_rows, part_rows)

    def hops(side, q):
        long = (q < PARTS // 2) == (side == 0)
        return 4 if long else 3

    def link(side, k, q, src):
        return sent(
            src,
            chain.at[side, k - 1, :, rows(q), :],
            sems.at[0, side, k - 1, q],
            sems.at[1, side, k - 1, q],
            place.id(z=place.along(sides[side])),
        )

    partial(place.along(4))
    for q in range(PARTS):
        for side in range(2):
            if hops(side, q) == 4:
                link(side, 4, q, pbuf.at[place.along(4), :, rows(q), :]).start()
    for k in (3, 2, 1):
        for side in range(2):
            partial(place.along(k * sides[side]))
            if k == 3:
                j = place.along(k * sides[side])
                for q in range(PARTS):
                    if hops(side, q) == 3:
                        link(side, 3, q, pbuf.at[j, :, rows(q), :]).start()
        for q in range(PARTS):
            for side in range(2):
                j = place.along(k * sides[side])
                if hops(side, q) == 3 and k == 3:
                    continue
                slot = chain.at[side, k, :, rows(q), :]
                link(side, k + 1, q, slot).wait_recv()
                chain[side, k, :, rows(q), :] = (
                    chain[side, k, :, rows(q), :].astype(F32) + pbuf[j, :, rows(q), :].astype(F32)
                ).astype(BF16)
                link(side, k, q, slot).start()
    partial(place.z)
    for q in range(PARTS):
        for side in range(2):
            slot = chain.at[side, 0, :, rows(q), :]
            link(side, 1, q, slot).wait_recv()
    for q in range(PARTS):
        for side in range(2):
            for k in range(1, hops(side, q) + 1):
                link(side, k, q, chain.at[side, k - 1, :, rows(q), :]).wait_send()


def spread_along_z(place, blocks, sems, on_arrival):
    half = MODAL_BLOCK // 2
    sides = (1, -1)

    def link(side, k, q, owner):
        rows = blocks.at[owner, pl.ds(q * half, half), :]
        return sent(
            rows, rows, sems.at[0, side, k - 1, q], sems.at[1, side, k - 1, q],
            place.id(z=place.along(sides[side])),
        )

    def used(side, k, q):
        return k < 4 or q == side

    for q in range(2):
        for side in range(2):
            link(side, 1, q, place.z).start()
    on_arrival(place.z)
    for k in (1, 2, 3, 4):
        for q in range(2):
            for side in range(2):
                if used(side, k, q):
                    owner = place.along(-k * sides[side])
                    link(side, k, q, owner).wait_recv()
                    if k < 4 and used(side, k + 1, q):
                        link(side, k + 1, q, owner).start()
        if k < 4:
            for side in range(2):
                on_arrival(place.along(-k * sides[side]))
        else:
            on_arrival(place.along(4))
    for k in (1, 2, 3, 4):
        for q in range(2):
            for side in range(2):
                if used(side, k, q):
                    link(side, k, q, place.along(-(k - 1) * sides[side])).wait_send()


def as_row(column):
    return jnp.transpose(jnp.broadcast_to(column, (MODAL_BLOCK, MODAL_BLOCK)))[:8]


def as_column(row):
    return jnp.transpose(jnp.broadcast_to(row, (MODAL_BLOCK, MODAL_BLOCK)))[:, :1]


def ffn_kernel(
    towers,
    residual,
    gain_own,
    gain_other,
    gate_own,
    gate_other,
    up_own,
    up_other,
    down_own,
    down_other,
    out,
    src,
    xg,
    wg0,
    wg1,
    wu0,
    wu1,
    wd0,
    wd1,
    pbuf,
    chain,
    ssp,
    ssr,
    acts,
    part,
    dbuf,
    rbuf,
    wsem,
    gsem,
    csem,
    ssem,
    asem,
    rsem,
):
    place = Place()
    loads = [
        pltpu.make_async_copy(a, b, wsem.at[k])
        for k, (a, b) in enumerate(
            ((gate_own, wg0), (gate_other, wg1), (up_own, wu0), (up_other, wu1), (down_own, wd0), (down_other, wd1))
        )
    ]
    for load in loads:
        load.start()
    src[...] = residual[...].astype(BF16)
    greet(place, [place.partner()] + [place.id(z=place.along(k)) for k in range(1, NZ)])
    gather_rows(place, src, xg, gsem)
    for load in loads[:4]:
        load.wait()

    def squares_to(k):
        j = place.along(k)
        return sent(
            ssp.at[j], ssr.at[place.z], ssem.at[0, k], ssem.at[1, k], place.id(z=j)
        )

    def partial(j):
        tower = towers[2 * j + place.l]
        x0 = xg[place.l, j].astype(F32)
        x1 = xg[1 - place.l, j].astype(F32)
        ssp[j] = as_row(
            jnp.sum(x0 * x0, axis=1, keepdims=True) + jnp.sum(x1 * x1, axis=1, keepdims=True)
        )
        n0 = (x0 * gain_own[tower]).astype(BF16)
        n1 = (x1 * gain_other[tower]).astype(BF16)
        for side, (w0, w1) in enumerate(((wg0, wg1), (wu0, wu1))):
            pbuf[j, side] = (
                jnp.dot(n0, w0[tower], preferred_element_type=F32)
                + jnp.dot(n1, w1[tower], preferred_element_type=F32)
            ).astype(BF16)

    sum_along_z(place, partial, pbuf, chain, csem)
    for k in range(1, NZ):
        squares_to(k).start()
    both = (
        pbuf[place.z].astype(F32) + chain[0, 0].astype(F32) + chain[1, 0].astype(F32)
    )
    squares = ssp[place.z]
    for k in range(1, NZ):
        slot = ssr.at[place.along(-k)]
        sent(slot, slot, ssem.at[0, k], ssem.at[1, k], place.id(z=place.along(k))).wait_recv()
        squares = squares + ssr[place.along(-k)]
    scale = as_column(lax.rsqrt(squares[:1] / D + EPSILON))
    gate = both[0] * scale
    up = both[1] * scale
    acts[place.z] = (gate / (1.0 + jnp.exp(-gate)) * up).astype(BF16)
    for load in loads[4:]:
        load.wait()

    def downward(j):
        tower = towers[2 * j + place.l]
        act = acts[j]
        part[place.l, j] = jnp.dot(act, wd0[tower], preferred_element_type=F32).astype(BF16)
        part[1 - place.l, j] = jnp.dot(act, wd1[tower], preferred_element_type=F32).astype(BF16)

    spread_along_z(place, acts, asem, downward)
    total = reduce_rows(place, part, dbuf, rbuf, rsem)
    out[...] = (residual[...] + total).astype(BF16)
    gather_rows_end(place, src, xg, gsem)
    for k in range(1, NZ):
        squares_to(k).wait_send()


def ffn(towers, residual, gains, gate, up, down):
    def other(value):
        return lax.ppermute(value, "yl", [(0, 1), (1, 0)])

    gains = gains[:, None, :]
    width = gate.shape[2]
    feats = gate.shape[1]
    vmem = pl.BlockSpec(memory_space=pltpu.VMEM)
    hbm = pl.BlockSpec(memory_space=pltpu.HBM)
    smem = pl.BlockSpec(memory_space=pltpu.SMEM)
    dma = pltpu.SemaphoreType.DMA
    return pl.pallas_call(
        ffn_kernel,
        out_shape=jax.ShapeDtypeStruct((MODAL_BLOCK, feats), BF16),
        in_specs=[smem, vmem, vmem, vmem] + [hbm] * 6,
        out_specs=vmem,
        scratch_shapes=[
            pltpu.VMEM((MODAL_BLOCK, feats), BF16),
            pltpu.VMEM((2, NB, MODAL_BLOCK, feats), BF16),
            pltpu.VMEM((2, feats, width), BF16),
            pltpu.VMEM((2, feats, width), BF16),
            pltpu.VMEM((2, feats, width), BF16),
            pltpu.VMEM((2, feats, width), BF16),
            pltpu.VMEM((2, width, feats), BF16),
            pltpu.VMEM((2, width, feats), BF16),
            pltpu.VMEM((NZ, 2, MODAL_BLOCK, width), BF16),
            pltpu.VMEM((2, 4, 2, MODAL_BLOCK, width), BF16),
            pltpu.VMEM((NZ, 8, MODAL_BLOCK), F32),
            pltpu.VMEM((NZ, 8, MODAL_BLOCK), F32),
            pltpu.VMEM((NZ, MODAL_BLOCK, width), BF16),
            pltpu.VMEM((2, NB, MODAL_BLOCK, feats), BF16),
            pltpu.VMEM((NB, MODAL_BLOCK, feats), BF16),
            pltpu.VMEM((NB, MODAL_BLOCK, feats), BF16),
            dma((6,)),
            dma((4, NB)),
            dma((2, 2, 4, PARTS)),
            dma((2, NZ)),
            dma((2, 2, 4, 2)),
            dma((4, NB)),
        ],
        compiler_params=pltpu.CompilerParams(collective_id=0, has_side_effects=True),
        name="ffn",
    )(towers, residual, gains, other(gains), gate, other(gate), up, other(up), down, other(down))


def local(tokens, modality, attn_gain, ffn_gain, w_query, w_keyval, w_out, w_gate, w_up, w_down):
    row_count = tokens.shape[0]
    total_rows = row_count * lax.axis_size(ROWS)
    share_rows = total_rows // lax.axis_size(MP)
    row_index = lax.axis_index(ROWS)
    mp_index = lax.axis_index(MP)
    own_towers = lax.dynamic_slice_in_dim(modality, row_index * row_count, row_count)
    hidden = tokens.astype(jnp.float32)
    squares = over_copies(jnp.sum(hidden * hidden, axis=1), MP)
    normed = scaled_rows(hidden, squares, attn_gain, own_towers)
    normed_all = gather_directly(normed, ROWS, 0)
    joint_weight = jnp.concatenate((w_query, w_keyval), axis=2)
    picked = normed_all
    projected = sent_and_summed(
        tower_rows(picked, joint_weight, block_towers(modality)).astype(jnp.bfloat16), MP, 0
    ).astype(jnp.bfloat16)
    query_width = w_query.shape[2]
    heads_here = query_width // HD
    queries = projected[:, :query_width].reshape(share_rows, heads_here, HD)
    keyval_local = projected[:, query_width:]
    head_group = row_index * heads_here // (HEADS // KV)
    keyval_block = gather_directly(keyval_local, ROWS, 1)
    keyval_all = gather_directly(pick_group(keyval_block, head_group), MP, 0)
    scores = jnp.einsum(
        "qhd,kd->hqk", queries, keyval_all[:, :HD], preferred_element_type=jnp.float32
    ) * HD ** (-0.5)
    query_pos = mp_index * share_rows + jnp.arange(share_rows, dtype=jnp.int32)
    key_pos = jnp.arange(total_rows, dtype=jnp.int32)
    allowed = key_pos[None, :] <= query_pos[:, None]
    scores = jnp.where(allowed[None, :, :], scores, -1e30)
    largest = jnp.max(scores, axis=2, keepdims=True)
    powers = jnp.exp(scores - largest)
    probs = (powers / jnp.sum(powers, axis=2, keepdims=True)).astype(jnp.bfloat16)
    context = jnp.einsum(
        "hqk,kd->qhd", probs, keyval_all[:, HD:], preferred_element_type=jnp.float32
    )
    context = context.astype(jnp.bfloat16).reshape(share_rows, query_width)
    context_all = gather_directly(context, MP, 0)
    picked = context_all
    residual = hidden + sent_and_summed(
        tower_rows(picked, w_out, block_towers(modality)).astype(jnp.bfloat16), ROWS, 0
    )
    return ffn(block_towers(modality), residual, ffn_gain, w_gate, w_up, w_down)


def solution(mesh):
    torus = Mesh(mesh.devices.reshape(NX, NYH, 2, 2, NZ), AXES)
    in_specs = (
        P(ROWS, MP),
        P(),
        P(None, MP),
        P(None, MP),
        P(None, MP, ROWS),
        P(None, MP, ROWS),
        P(None, ROWS, MP),
        P(None, MP, ROWS),
        P(None, MP, ROWS),
        P(None, ROWS, MP),
    )
    out_specs = P(ROWS, MP)
    return jax.shard_map(local, mesh=torus, in_specs=in_specs, out_specs=out_specs, check_vma=False)
```

time: 397 us -> 277 us (0.70)
  waiting for transfers between devices: 217 us -> 94.9 us
  Pallas kernels: 0 us -> 78.1 us
  blocking collectives: 103 us -> 43.8 us
  between operations: 13.4 us -> 0.29 us
  matrix products: 9.48 us -> 2.43 us
  starting transfers between devices: 31.6 us -> 36.7 us
    pallas_call x0 -> x1, Pallas kernels: none -> 78.1 us  [ffn(): pl.pallas_call(ffn_kernel, out_shape=jax.ShapeDtypeStruct((MODAL_BLOCK, f...]
    reduce_scatter x2 -> x0, waiting for transfers between devices: 77.3 us -> none  [reduced_to_own(): blocks = lax.psum_scatter(blocks, axes[k], scatter_dimension=0, tiled=True)]
    all_gather x1 -> x0, waiting for transfers between devices: 75.6 us -> none  [local(): activated_all = lax.all_gather(activated, MP, axis=0, tiled=True)]
    all_to_all x3 -> x1, blocking collectives: 64.2 us -> 24 us  [sent_and_summed(): lax.all_to_all(blocks, axis, split_axis=0, concat_axis=0, tiled=True)]
    ppermute x0 -> x4, waiting for transfers between devices: none -> 39.6 us  [other(): return lax.ppermute(value, 'yl', [(0, 1), (1, 0)])]
    all_to_all x2 -> x1, blocking collectives: 39.1 us -> 19.8 us  [from_everyone(): return lax.all_to_all(copies, axis, split_axis=0, concat_axis=0, tiled=True)]
    all_to_all x5 -> x4, waiting for transfers between devices: 63.7 us -> 55.3 us  [from_everyone(): return lax.all_to_all(copies, axis, split_axis=0, concat_axis=0, tiled=True)]
    all_to_all x0 -> x1, starting transfers between devices: none -> 5.65 us  [sent_and_summed(): lax.all_to_all(blocks, axis, split_axis=0, concat_axis=0, tiled=True)]
  transfers between devices with their start and end apart: 8 -> 9, of which waited for: 8 -> 6; matrix products, arithmetic and copies ran while one was open for 0% -> 3% of each run, Pallas kernels for 0% -> 0%
where the time goes in v1:
time: 277 us; the launch traced here: 274 us
  waiting for transfers between devices  94.9 us (34%)
  Pallas kernels  78.1 us (28%)
  blocking collectives  43.8 us (16%)
  starting transfers between devices  36.7 us (13%)
  local copies, waits for them, and re-layouts  13.8 us (5%)
  other arithmetic  4.16 us (2%)
    pallas_call x1, Pallas kernels, ffn(): pl.pallas_call(ffn_kernel, out_shape=jax.ShapeDtypeStruct((MODAL_BLOCK, f...  78.1 us
    all_to_all x4, waiting for transfers between devices, from_everyone(): return lax.all_to_all(copies, axis, split_axis=0, concat_axis=0, tiled=True)  55.3 us
    ppermute x4, waiting for transfers between devices, other(): return lax.ppermute(value, 'yl', [(0, 1), (1, 0)])  39.6 us
    all_to_all x4, starting transfers between devices, from_everyone(): return lax.all_to_all(copies, axis, split_axis=0, concat_axis=0, tiled=True)  27 us
    all_to_all x1, blocking collectives, sent_and_summed(): lax.all_to_all(blocks, axis, split_axis=0, concat_axis=0, tiled=True)  24 us
    all_to_all x1, blocking collectives, from_everyone(): return lax.all_to_all(copies, axis, split_axis=0, concat_axis=0, tiled=True)  19.8 us
    all_to_all x1, starting transfers between devices, sent_and_summed(): lax.all_to_all(blocks, axis, split_axis=0, concat_axis=0, tiled=True)  5.65 us
  transfers between devices with their start and end apart: 9, of which 6 were waited for; matrix products, arithmetic and copies ran while one was open for 3% of the time, Pallas kernels for 0%

profile of v1, /device:TPU:4, one launch (start us, length us, event | category | flops | bytes accessed | tf_op | source)
XLA Modules:
  0.0 274.2 jit_solution(6780158471277086721)
XLA Ops:
  0.0 0.9 multiply_reduce_fusion
  0.9 0.6 broadcast_in_dim.105
  1.5 9.6 %all-to-all-start = ((f32[16,1,128]{2,1,0:T(1,128)}), f32[16,1,128]{2,1,0:T(1,128)S(1)}, u32[]{:S(2)}, u32[]{:S(2)}) async-start(f32[16,1,128]{2,1,0:T(1,128)} %broadcast_in_dim.105), calls=%async_computation | async-start | bytes 16384 | tf_op jit(solution)/shard_map/all_to_all | solution.py:29
  11.1 0.8 fusion.30
  11.9 0.8 dynamic-slice_compare_fusion
  12.6 6.9 %all-to-all-done = f32[16,1,128]{2,1,0:T(1,128)S(1)} async-done(((f32[16,1,128]{2,1,0:T(1,128)}), f32[16,1,128]{2,1,0:T(1,128)S(1)}, u32[]{:S(2)}, u32[]{:S(2)}) %all-to-all-start) | async-done | bytes 8224 | tf_op jit(solution)/shard_map/all_to_all | solution.py:29
  19.5 0.9 multiply_convert_fusion
  20.5 1.0 broadcast_in_dim.111
  21.5 7.2 %all-to-all-start.1 = ((bf16[16,128,224]{1,2,0:T(8,128)(2,1)}), bf16[16,128,224]{1,2,0:T(8,128)(2,1)S(1)}, u32[]{:S(2)}, u32[]{:S(2)}) async-start(bf16[16,128,224]{1,2,0:T(8,128)(2,1)} %broadcast_in_dim.111), calls=%async_computation.1 | async-start | bytes 1835008 | tf_op jit(solution)/shard_map/all_to_all | solution.py:29
  28.7 0.1 copy.88
  28.8 0.1 slice_reduce_fusion.towers
  29.0 14.0 %all-to-all-done.1 = bf16[16,128,224]{1,2,0:T(8,128)(2,1)S(1)} async-done(((bf16[16,128,224]{1,2,0:T(8,128)(2,1)}), bf16[16,128,224]{1,2,0:T(8,128)(2,1)S(1)}, u32[]{:S(2)}, u32[]{:S(2)}) %all-to-all-start.1) | async-done | bytes 917536 | tf_op jit(solution)/shard_map/all_to_all | solution.py:29
  42.9 0.2 select_bitcast_fusion
  43.1 0.4 fusion.10
  43.6 0.4 fusion.5
  44.0 0.2 copy.116
  44.2 24.0 %all_to_all.36 = bf16[16,128,192]{1,2,0:T(8,128)(2,1)S(1)} all-to-all(bf16[16,128,192]{1,2,0:T(8,128)(2,1)S(1)} %bitcast.59), channel_id=1, replica_groups=mesh['x'=4,'yh'=2,'c'=2,'yl'=2,'z'=8] {'yl','z'}, dimensions={0} | all-to-all | bytes 1572864 | tf_op jit(solution)/shard_map/all_to_all | solution.py:55
  68.2 0.1 reduce_sum.50
  68.3 0.8 broadcast_in_dim.112
  69.1 5.9 %all-to-all-start.3 = ((bf16[16,128,64]{1,2,0:T(8,128)(2,1)}), bf16[16,128,64]{1,2,0:T(8,128)(2,1)S(1)}, u32[]{:S(2)}, u32[]{:S(2)}) async-start(bf16[16,128,64]{1,2,0:T(8,128)(2,1)} %broadcast_in_dim.112), calls=%async_computation.3 | async-start | bytes 524288 | tf_op jit(solution)/shard_map/all_to_all | solution.py:29
  75.0 6.9 %all-to-all-done.3 = bf16[16,128,64]{1,2,0:T(8,128)(2,1)S(1)} async-done(((bf16[16,128,64]{1,2,0:T(8,128)(2,1)}), bf16[16,128,64]{1,2,0:T(8,128)(2,1)S(1)}, u32[]{:S(2)}, u32[]{:S(2)}) %all-to-all-start.3) | async-done | bytes 262176 | tf_op jit(solution)/shard_map/all_to_all | solution.py:29
  82.0 1.1 broadcast_in_dim.113
  83.1 4.4 %all-to-all-start.4 = ((bf16[16,128,256]{2,1,0:T(8,128)(2,1)}), bf16[16,128,256]{2,1,0:T(8,128)(2,1)S(1)}, u32[]{:S(2)}, u32[]{:S(2)}) async-start(bf16[16,128,256]{2,1,0:T(8,128)(2,1)} %broadcast_in_dim.113), calls=%async_computation.4 | async-start | bytes 2097152 | tf_op jit(solution)/shard_map/all_to_all | solution.py:29
  87.5 27.5 %all-to-all-done.4 = bf16[16,128,256]{2,1,0:T(8,128)(2,1)S(1)} async-done(((bf16[16,128,256]{2,1,0:T(8,128)(2,1)}), bf16[16,128,256]{2,1,0:T(8,128)(2,1)S(1)}, u32[]{:S(2)}, u32[]{:S(2)}) %all-to-all-start.4) | async-done | bytes 1048608 | tf_op jit(solution)/shard_map/all_to_all | solution.py:29
  115.1 0.4 fusion.31
  115.5 0.3 fusion.7
  115.8 0.4 fusion.6
  116.4 19.8 %all_to_all.37 = bf16[16,128,128]{2,1,0:T(8,128)(2,1)S(1)} all-to-all(bf16[16,128,128]{2,1,0:T(8,128)(2,1)S(1)} %broadcast_in_dim.115), channel_id=1, replica_groups=mesh['x'=4,'yh'=2,'c'=2,'yl'=2,'z'=8] {'yl','z'}, dimensions={0} | all-to-all | bytes 1048576 | tf_op jit(solution)/shard_map/all_to_all | solution.py:29
  136.2 0.1 broadcast_select_fusion
  136.3 0.4 fusion.23
  136.7 0.4 fusion.4
  137.2 1.1 copy.115
  138.3 5.7 %all-to-all-start.6 = ((bf16[16,128,224]{1,2,0:T(8,128)(2,1)}), bf16[16,128,224]{1,2,0:T(8,128)(2,1)S(1)}, u32[]{:S(2)}, u32[]{:S(2)}) async-start(bf16[16,128,224]{1,2,0:T(8,128)(2,1)} %bitcast.57), calls=%async_computation.6 | async-start | bytes 1835008 | tf_op jit(solution)/shard_map/all_to_all | solution.py:55
  143.9 1.0 collective-permute-start.3
  145.0 1.0 collective-permute-start.1
  146.0 1.0 collective-permute-start.2
  147.0 1.0 collective-permute-start
  148.1 2.1 copy.97.down_own
  150.2 18.7 %collective-permute-done.3 = bf16[2,592,224]{1,2,0:T(8,128)(2,1)} collective-permute-done((bf16[2,592,224]{1,2,0:T(8,128)(2,1)}, bf16[2,592,224]{1,2,0:T(8,128)(2,1)}, u32[]{:S(2)}, u32[]{:S(2)}) %collective-permute-start.3) | collective-permute-done | bytes 530464 | tf_op jit(solution)/shard_map/ppermute | solution.py:445
  168.9 2.1 copy.98.down_other
  171.1 0.1 convert_reduce_fusion
  171.3 0.7 add.62.residual
  172.0 20.9 %collective-permute-done.gain_other = f32[2,1,224]{2,1,0:T(1,128)S(1)} collective-permute-done((f32[2,1,224]{2,1,0:T(1,128)S(1)}, f32[2,1,224]{2,1,0:T(1,128)S(1)}, u32[]{:S(2)}, u32[]{:S(2)}) %collective-permute-start) | collective-permute-done | bytes 1824 | tf_op jit(solution)/shard_map/ppermute | solution.py:445
  192.9 0.5 copy-done.10
  193.5 0.3 copy-done.2
  193.7 0.8 copy-done.3
  194.5 78.1 %ffn.1 = bf16[128,224]{1,0:T(8,128)(2,1)} custom-call(s32[16]{0:T(128)} %copy-done.11, f32[128,224]{1,0:T(8,128)} %add.62.residual, f32[2,1,224]{2,1,0:T(1,128)} %copy-done.8, f32[2,1,224]{2,1,0:T(1,128)} %copy-done.10, bf16[2,224,592]{2,1,0:T(8,128)(2,1)} %gate_own.1, bf16[2,224,592]{2,1,0:T(8,128)(2,1)} %copy-done.2, bf16[2,224,592]{2,1,0:T(8,128)(2,1)} %up_own.1, ...), custom_call_target="tpu_custom_call" | custom-call | tf_op jit(solution)/shard_map/ffn/pallas_call | solution.py:454
  272.6 1.6 copy.99
  (39 shorter events, 0.6 us)
Async XLA Ops:
  0.0 28.8 %copy-start.9 = (s32[2048]{0:T(1024)S(1)}, s32[2048]{0:T(1024)}, u32[]{:S(2)}) copy-start(s32[2048]{0:T(1024)} %param.11) | copy-start | bytes 24580
  0.0 28.7 %copy-start.7 = (bf16[2,224,64]{1,2,0:T(8,128)(2,1)S(1)}, bf16[2,224,64]{1,2,0:T(8,128)(2,1)}, u32[]{:S(2)}) copy-start(bf16[2,224,64]{1,2,0:T(8,128)(2,1)} %param.15) | copy-start | bytes 172036
  1.5 18.0 %all-to-all-start = ((f32[16,1,128]{2,1,0:T(1,128)}), f32[16,1,128]{2,1,0:T(1,128)S(1)}, u32[]{:S(2)}, u32[]{:S(2)}) async-start(f32[16,1,128]{2,1,0:T(1,128)} %broadcast_in_dim.105), calls=%async_computation | async-start | bytes 16384 | tf_op jit(solution)/shard_map/all_to_all | solution.py:29
  21.5 21.4 %all-to-all-start.1 = ((bf16[16,128,224]{1,2,0:T(8,128)(2,1)}), bf16[16,128,224]{1,2,0:T(8,128)(2,1)S(1)}, u32[]{:S(2)}, u32[]{:S(2)}) async-start(bf16[16,128,224]{1,2,0:T(8,128)(2,1)} %broadcast_in_dim.111), calls=%async_computation.1 | async-start | bytes 1835008 | tf_op jit(solution)/shard_map/all_to_all | solution.py:29
  28.7 14.4 %copy-start.5 = (bf16[2,224,128]{2,1,0:T(8,128)(2,1)S(1)}, bf16[2,224,128]{2,1,0:T(8,128)(2,1)}, u32[]{:S(2)}) copy-start(bf16[2,224,128]{2,1,0:T(8,128)(2,1)} %param.14) | copy-start | bytes 344068
  28.9 14.6 %copy-start.11 = (s32[16]{0:T(128)}, s32[16]{0:T(128)S(1)}, u32[]{:S(2)}) copy-start(s32[16]{0:T(128)S(1)} %slice_reduce_fusion.towers) | copy-start | bytes 196
  69.1 12.8 %all-to-all-start.3 = ((bf16[16,128,64]{1,2,0:T(8,128)(2,1)}), bf16[16,128,64]{1,2,0:T(8,128)(2,1)S(1)}, u32[]{:S(2)}, u32[]{:S(2)}) async-start(bf16[16,128,64]{1,2,0:T(8,128)(2,1)} %broadcast_in_dim.112), calls=%async_computation.3 | async-start | bytes 524288 | tf_op jit(solution)/shard_map/all_to_all | solution.py:29
  83.1 32.0 %all-to-all-start.4 = ((bf16[16,128,256]{2,1,0:T(8,128)(2,1)}), bf16[16,128,256]{2,1,0:T(8,128)(2,1)S(1)}, u32[]{:S(2)}, u32[]{:S(2)}) async-start(bf16[16,128,256]{2,1,0:T(8,128)(2,1)} %broadcast_in_dim.113), calls=%async_computation.4 | async-start | bytes 2097152 | tf_op jit(solution)/shard_map/all_to_all | solution.py:29
  116.2 20.2 %copy-start.6 = (bf16[2,128,224]{1,2,0:T(8,128)(2,1)S(1)}, bf16[2,128,224]{1,2,0:T(8,128)(2,1)}, u32[]{:S(2)}) copy-start(bf16[2,128,224]{1,2,0:T(8,128)(2,1)} %param.16) | copy-start | bytes 344068
  137.2 7.8 %copy-start = (bf16[2,224,592]{2,1,0:T(8,128)(2,1)S(1)}, bf16[2,224,592]{2,1,0:T(8,128)(2,1)}, u32[]{:S(2)}) copy-start(bf16[2,224,592]{2,1,0:T(8,128)(2,1)} %gate_own.1) | copy-start | bytes 1591300
  137.2 8.8 %copy-start.1 = (bf16[2,224,592]{2,1,0:T(8,128)(2,1)S(1)}, bf16[2,224,592]{2,1,0:T(8,128)(2,1)}, u32[]{:S(2)}) copy-start(bf16[2,224,592]{2,1,0:T(8,128)(2,1)} %up_own.1) | copy-start | bytes 1591300
  137.2 9.8 %copy-start.12 = (f32[2,224]{1,0:T(2,128)S(1)}, f32[2,224]{1,0:T(2,128)}, u32[]{:S(2)}) copy-start(f32[2,224]{1,0:T(2,128)} %param.13) | copy-start | bytes 5380
  137.2 10.8 %copy-start.4 = (bf16[128,224]{0,1:T(8,128)(2,1)S(1)}, bf16[128,224]{0,1:T(8,128)(2,1)}, u32[]{:S(2)}) copy-start(bf16[128,224]{0,1:T(8,128)(2,1)} %param.10) | copy-start | bytes 172036
  138.3 32.8 %all-to-all-start.6 = ((bf16[16,128,224]{1,2,0:T(8,128)(2,1)}), bf16[16,128,224]{1,2,0:T(8,128)(2,1)S(1)}, u32[]{:S(2)}, u32[]{:S(2)}) async-start(bf16[16,128,224]{1,2,0:T(8,128)(2,1)} %bitcast.57), calls=%async_computation.6 | async-start | bytes 1835008 | tf_op jit(solution)/shard_map/all_to_all | solution.py:55
  143.9 25.0 %collective-permute-start.3 = (bf16[2,592,224]{1,2,0:T(8,128)(2,1)}, bf16[2,592,224]{1,2,0:T(8,128)(2,1)}, u32[]{:S(2)}, u32[]{:S(2)}) collective-permute-start(bf16[2,592,224]{1,2,0:T(8,128)(2,1)} %param.19), channel_id=1, source_target_pairs={{0,8},{8,0},{1,9},{9,1},{2,10},{10,2},{3,11},{11,3},{4,12},{12,4},... | collective-permute-start | bytes 1591304 | tf_op jit(solution)/shard_map/ppermute | solution.py:445
  145.0 47.9 %collective-permute-start.1 = (bf16[2,224,592]{2,1,0:T(8,128)(2,1)S(1)}, bf16[2,224,592]{2,1,0:T(8,128)(2,1)S(1)}, u32[]{:S(2)}, u32[]{:S(2)}) collective-permute-start(bf16[2,224,592]{2,1,0:T(8,128)(2,1)S(1)} %copy-done), channel_id=1, source_target_pairs={{0,8},{8,0},{1,9},{9,1},{2,10},{10,2},{3,11},{11,3},{4,12},{12,4},... | collective-permute-start | bytes 1591304 | tf_op jit(solution)/shard_map/ppermute | solution.py:445
  146.0 46.9 %collective-permute-start.2 = (bf16[2,224,592]{2,1,0:T(8,128)(2,1)S(1)}, bf16[2,224,592]{2,1,0:T(8,128)(2,1)S(1)}, u32[]{:S(2)}, u32[]{:S(2)}) collective-permute-start(bf16[2,224,592]{2,1,0:T(8,128)(2,1)S(1)} %copy-done.1), channel_id=1, source_target_pairs={{0,8},{8,0},{1,9},{9,1},{2,10},{10,2},{3,11},{11,3},{4,12},{12,4},... | collective-permute-start | bytes 1591304 | tf_op jit(solution)/shard_map/ppermute | solution.py:445
  147.0 24.3 %copy-start.8 = (f32[2,1,224]{2,1,0:T(1,128)}, f32[2,1,224]{2,1,0:T(1,128)S(1)}, u32[]{:S(2)}) copy-start(f32[2,1,224]{2,1,0:T(1,128)S(1)} %broadcast_in_dim.116.gain_own) | copy-start | bytes 5380
  147.0 45.9 %collective-permute-start = (f32[2,1,224]{2,1,0:T(1,128)S(1)}, f32[2,1,224]{2,1,0:T(1,128)S(1)}, u32[]{:S(2)}, u32[]{:S(2)}) collective-permute-start(f32[2,1,224]{2,1,0:T(1,128)S(1)} %broadcast_in_dim.116.gain_own), channel_id=1, source_target_pairs={{0,8},{8,0},{1,9},{9,1},{2,10},{10,2},{3,11},{11,3},{4,12},{12,4},... | collective-permute-start | bytes 5384 | tf_op jit(solution)/shard_map/ppermute | solution.py:445
  192.9 0.6 copy-start.10
  192.9 0.8 copy-start.2
  193.7 0.8 copy-start.3

commit v2 on v1

v2 whole, which is shorter than its diff:
```python
import jax
import jax.numpy as jnp
from jax import lax
from jax.experimental import pallas as pl
from jax.experimental.pallas import tpu as pltpu
from jax.sharding import Mesh
from jax.sharding import PartitionSpec as P

D = 3584
HD = 128
MODAL_BLOCK = 128
ROWS = ("x", "yh", "c")
MP = ("yl", "z")
AXES = ("x", "yh", "c", "yl", "z")
NX, NYH, NZ = 4, 2, 8
NB = NX * NYH

EPSILON = 1e-06
F32 = jnp.float32
BF16 = jnp.bfloat16


class Place:
    def __init__(self):
        self.at = {a: lax.axis_index(a) for a in AXES}
        self.x, self.h, self.c, self.l, self.z = (self.at[a] for a in AXES)
        self.crossed = (self.c - self.l) * (self.c - self.l)
        xa, xb = self.x // NYH, lax.rem(self.x, NYH)
        self.moved = 1 - (1 - (xa - xb) * (xa - xb)) * (1 - (xb - self.h) * (xb - self.h))

    def id(self, **moved):
        return tuple(moved.get(a, self.at[a]) for a in AXES)

    def cross(self, dx, dh):
        return self.id(
            x=lax.rem(self.x + dx, NX), yh=lax.rem(self.h + dh, NYH), c=self.l, yl=self.c
        )

    def ahead(self, dx, dh):
        return NYH * lax.rem(self.x + dx, NX) + lax.rem(self.h + dh, NYH)

    def behind(self, dx, dh):
        return NYH * lax.rem(self.x - dx + NX, NX) + lax.rem(self.h - dh + NYH, NYH)

    def partner(self):
        return self.id(c=1 - self.c)

    def along(self, k):
        return lax.rem(self.z + k + NZ, NZ)

    def up_y(self):
        return lax.rem(self.h + self.l, NYH), 1 - self.l

    def down_y(self):
        return lax.rem(self.h + 1 - self.l, NYH), 1 - self.l

    def keyval_to(self):
        return NYH * lax.rem(self.x, NYH) + self.h, self.x // NYH

    def keyval_from(self):
        return NYH * self.h + self.x // NYH, lax.rem(self.x, NYH)


OFFSETS = tuple((dx, dh) for dx in (2, 1, 3, 0) for dh in (1, 0))


def sent(src, dst, send, recv, target):
    return pltpu.make_async_remote_copy(
        src_ref=src,
        dst_ref=dst,
        send_sem=send,
        recv_sem=recv,
        device_id=target,
        device_id_type=pl.DeviceIdType.MESH,
    )


def greet(place, peers):
    barrier = pltpu.get_barrier_semaphore()

    def hello(peer):
        pl.semaphore_signal(barrier, 1, device_id=peer, device_id_type=pl.DeviceIdType.MESH)

    count = 0
    for peer in peers + [place.cross(*o) for o in OFFSETS if o != (0, 0)]:
        hello(peer)
        count += 1
    xs, hs = place.keyval_from()
    for k in range(1, NZ):
        hello(place.id(x=xs, yh=hs, z=place.along(k)))
        count += 1
    pl.when(place.c != place.l)(lambda: hello(place.cross(0, 0)))
    pl.when(place.moved != 0)(lambda: hello(place.id(x=xs, yh=hs)))
    pl.semaphore_wait(barrier, count + place.crossed + place.moved)


def gather_rows(place, src, xg, sems):
    send, recv, fsend, frecv = (sems.at[k] for k in range(4))
    own = NYH * place.x + place.h
    for i, (dx, dh) in enumerate(OFFSETS):
        copy = sent(src, xg.at[place.l, own], send.at[i], recv.at[i], place.cross(dx, dh))
        if (dx, dh) != (0, 0):
            copy.start()
        else:
            pl.when(place.c != place.l)(copy.start)

            @pl.when(place.c == place.l)
            def _():
                xg[place.l, own] = src[...]

    order = sorted(range(NB), key=lambda i: (min(OFFSETS[i][0], NX - OFFSETS[i][0]), OFFSETS[i][1]))
    for i in order:
        dx, dh = OFFSETS[i]
        slot = xg.at[place.c, place.behind(dx, dh)]
        arrive = sent(slot, slot, send.at[i], recv.at[i], place.cross(dx, dh))
        if (dx, dh) != (0, 0):
            arrive.wait_recv()
        else:
            pl.when(place.c != place.l)(arrive.wait_recv)
        sent(slot, slot, fsend.at[i], frecv.at[i], place.partner()).start()
    for i in order:
        dx, dh = OFFSETS[i]
        slot = xg.at[1 - place.c, place.behind(dx, dh)]
        sent(slot, slot, fsend.at[i], frecv.at[i], place.partner()).wait_recv()


def gather_rows_end(place, src, xg, sems):
    send, recv, fsend, frecv = (sems.at[k] for k in range(4))
    for i, (dx, dh) in enumerate(OFFSETS):
        copy = sent(src, src, send.at[i], recv.at[i], place.cross(dx, dh))
        if (dx, dh) != (0, 0):
            copy.wait_send()
        else:
            pl.when(place.c != place.l)(copy.wait_send)
        slot = xg.at[place.c, place.behind(dx, dh)]
        sent(slot, slot, fsend.at[i], frecv.at[i], place.partner()).wait_send()


def reduce_rows(place, part, dbuf, rbuf, sems):
    send, recv, fsend, frecv = (sems.at[k] for k in range(4))
    own = NYH * place.x + place.h
    for i, (dx, dh) in enumerate(OFFSETS):
        j = place.ahead(dx, dh)
        sent(
            part.at[1 - place.c, j], dbuf.at[j], fsend.at[i], frecv.at[i], place.partner()
        ).start()
    for i, (dx, dh) in enumerate(OFFSETS):
        j = place.ahead(dx, dh)
        sent(part.at[1 - place.c, j], dbuf.at[j], fsend.at[i], frecv.at[i], place.partner()).wait_recv()
        total = part[place.c, j].astype(F32) + dbuf[j].astype(F32)
        dbuf[j] = total.astype(BF16)
        copy = sent(dbuf.at[j], rbuf.at[i], send.at[i], recv.at[i], place.cross(dx, dh))
        if (dx, dh) != (0, 0):
            copy.start()
        else:
            pl.when(place.c != place.l)(copy.start)

            @pl.when(place.c == place.l)
            def _():
                rbuf[i] = dbuf[own]

    total = None
    order = sorted(range(NB), key=lambda i: (min(OFFSETS[i][0], NX - OFFSETS[i][0]), OFFSETS[i][1]))
    for i in order:
        dx, dh = OFFSETS[i]
        arrive = sent(rbuf.at[i], rbuf.at[i], send.at[i], recv.at[i], place.cross(dx, dh))
        if (dx, dh) != (0, 0):
            arrive.wait_recv()
        else:
            pl.when(place.c != place.l)(arrive.wait_recv)
        term = rbuf[i].astype(F32)
        total = term if total is None else total + term
    for i, (dx, dh) in enumerate(OFFSETS):
        j = place.ahead(dx, dh)
        sent(part.at[1 - place.c, j], dbuf.at[j], fsend.at[i], frecv.at[i], place.partner()).wait_send()
        copy = sent(dbuf.at[j], rbuf.at[i], send.at[i], recv.at[i], place.cross(dx, dh))
        if (dx, dh) != (0, 0):
            copy.wait_send()
        else:
            pl.when(place.c != place.l)(copy.wait_send)
    return total


PARTS = 4


def sum_along_z(place, partial, pbuf, chain, sems):
    part_rows = MODAL_BLOCK // PARTS
    sides = (1, -1)

    def rows(q):
        return pl.ds(q * part_rows, part_rows)

    def hops(side, q):
        long = (q < PARTS // 2) == (side == 0)
        return 4 if long else 3

    def link(side, k, q, src):
        return sent(
            src,
            chain.at[side, k - 1, :, rows(q), :],
            sems.at[0, side, k - 1, q],
            sems.at[1, side, k - 1, q],
            place.id(z=place.along(sides[side])),
        )

    partial(place.along(4))
    for q in range(PARTS):
        for side in range(2):
            if hops(side, q) == 4:
                link(side, 4, q, pbuf.at[place.along(4), :, rows(q), :]).start()
    for k in (3, 2, 1):
        for side in range(2):
            partial(place.along(k * sides[side]))
            if k == 3:
                j = place.along(k * sides[side])
                for q in range(PARTS):
                    if hops(side, q) == 3:
                        link(side, 3, q, pbuf.at[j, :, rows(q), :]).start()
        for q in range(PARTS):
            for side in range(2):
                j = place.along(k * sides[side])
                if hops(side, q) == 3 and k == 3:
                    continue
                slot = chain.at[side, k, :, rows(q), :]
                link(side, k + 1, q, slot).wait_recv()
                chain[side, k, :, rows(q), :] = (
                    chain[side, k, :, rows(q), :].astype(F32) + pbuf[j, :, rows(q), :].astype(F32)
                ).astype(BF16)
                link(side, k, q, slot).start()
    partial(place.z)
    for q in range(PARTS):
        for side in range(2):
            slot = chain.at[side, 0, :, rows(q), :]
            link(side, 1, q, slot).wait_recv()
    for q in range(PARTS):
        for side in range(2):
            for k in range(1, hops(side, q) + 1):
                link(side, k, q, chain.at[side, k - 1, :, rows(q), :]).wait_send()


def spread_along_z(place, blocks, sems, on_arrival):
    half = MODAL_BLOCK // 2
    sides = (1, -1)

    def link(side, k, q, owner):
        rows = blocks.at[owner, pl.ds(q * half, half), :]
        return sent(
            rows, rows, sems.at[0, side, k - 1, q], sems.at[1, side, k - 1, q],
            place.id(z=place.along(sides[side])),
        )

    def used(side, k, q):
        return k < 4 or q == side

    for q in range(2):
        for side in range(2):
            link(side, 1, q, place.z).start()
    on_arrival(place.z)
    for k in (1, 2, 3, 4):
        for q in range(2):
            for side in range(2):
                if used(side, k, q):
                    owner = place.along(-k * sides[side])
                    link(side, k, q, owner).wait_recv()
                    if k < 4 and used(side, k + 1, q):
                        link(side, k + 1, q, owner).start()
        if k < 4:
            for side in range(2):
                on_arrival(place.along(-k * sides[side]))
        else:
            on_arrival(place.along(4))
    for k in (1, 2, 3, 4):
        for q in range(2):
            for side in range(2):
                if used(side, k, q):
                    link(side, k, q, place.along(-(k - 1) * sides[side])).wait_send()


def along_order():
    return (4, 3, 5, 2, 6, 1, 7)


def lhs_t(a, b):
    return lax.dot_general(a, b, (((0,), (0,)), ((), ())), preferred_element_type=F32)


def rhs_t(a, b):
    return lax.dot_general(a, b, (((1,), (1,)), ((), ())), preferred_element_type=F32)


def as_column(row):
    return jnp.transpose(jnp.broadcast_to(row, (MODAL_BLOCK, MODAL_BLOCK)))[:, :1]


def layer_kernel(
    towers, tokens, gains, wq_in, wkv_in, wo_in, wg_in, wu_in, wd_in,
    out,
    xa, gother, gcol, wq, wkv, wo, wg, wu, wd,
    qsend, kvsend, qrecv, kvrecv, ssa, ssar, kvown, kvall, scores, ctxs,
    parta, dbufa, rbufa, resid, src,
    xg, pbuf, chain, ssp, ssr, acts, part, dbuf, rbuf,
    lsem, wsem, ga_sem, q_sem, kv_sem, sa_sem, kz_sem, ky_sem, kr_sem, kd_sem, cx_sem, ra_sem,
    g_sem, c_sem, s_sem, a_sem, r_sem,
):
    place = Place()
    own = place.l
    oth = 1 - place.l
    loads = [
        pltpu.make_async_copy(a, b.at[0], lsem.at[k])
        for k, (a, b) in enumerate(
            ((wq_in, wq), (wkv_in, wkv), (wo_in, wo), (wg_in, wg), (wu_in, wu), (wd_in, wd))
        )
    ]
    for load in loads:
        load.start()
    xd, hd = place.keyval_to()
    xs, hs = place.keyval_from()
    uh, ul = place.up_y()
    dh, dl = place.down_y()
    above = place.id(yh=uh, yl=ul)
    below = place.id(yh=dh, yl=dl)
    twin = place.id(yl=1 - place.l)
    greet(
        place,
        [place.partner(), above, below] + [place.id(z=place.along(k)) for k in range(1, NZ)],
    )

    exchange = []
    for k, (a, b) in enumerate(
        [(gains, gother), (wq_in, wq.at[1]), (wkv_in, wkv.at[1]), (wo_in, wo.at[1])]
        + [(w.at[t], v.at[1, t]) for w, v in ((wg_in, wg), (wu_in, wu), (wd_in, wd)) for t in range(2)]
    ):
        exchange.append(sent(a, b, wsem.at[0, k], wsem.at[1, k], twin))

    for e in exchange[:3]:
        e.start()
    gather_rows(place, tokens, xa, ga_sem)
    exchange[3].start()
    exchange[4].start()

    for e in exchange[:3]:
        e.wait_recv()
    for t in range(2):
        for which in range(2):
            for piece, g in enumerate((gains, gother)):
                row = jnp.broadcast_to(g[which * 2 + t], (MODAL_BLOCK, g.shape[2]))
                gcol[which, piece, t] = jnp.transpose(row)
    for load in loads[:2]:
        load.wait()

    def q_copy(k):
        j = place.along(k)
        return sent(qsend.at[j], qrecv.at[place.z], q_sem.at[0, k], q_sem.at[1, k], place.id(z=j))

    def kv_copy(k):
        j = place.along(k)
        return sent(
            kvsend.at[j], kvrecv.at[place.z], kv_sem.at[0, k], kv_sem.at[1, k],
            place.id(x=xd, yh=hd, z=j),
        )

    def ssa_copy(k):
        j = place.along(k)
        return sent(ssa.at[j], ssar.at[place.z], sa_sem.at[0, k], sa_sem.at[1, k], place.id(z=j))

    def squares_of(x0, x1):
        row = jnp.sum(x0 * x0, axis=0, keepdims=True) + jnp.sum(x1 * x1, axis=0, keepdims=True)
        return jnp.broadcast_to(row, (8, MODAL_BLOCK))

    for k in along_order() + (0,):
        j = place.along(k)
        tower = towers[2 * j + place.l]
        x0 = xa[own, j].astype(F32)
        x1 = xa[oth, j].astype(F32)
        ssa[j] = squares_of(x0, x1)
        n0 = (x0 * gcol[0, 0, tower]).astype(BF16)
        n1 = (x1 * gcol[0, 1, tower]).astype(BF16)
        qsend[j] = (lhs_t(wq[0, tower], n0) + lhs_t(wq[1, tower], n1)).astype(BF16)
        kvsend[j] = (
            jnp.dot(wkv[0, tower], n0, preferred_element_type=F32)
            + jnp.dot(wkv[1, tower], n1, preferred_element_type=F32)
        ).astype(BF16)
        if k:
            kv_copy(k).start()
            q_copy(k).start()
            ssa_copy(k).start()
        else:
            pl.when(place.moved != 0)(kv_copy(0).start)

            @pl.when(place.moved == 0)
            def _():
                kvrecv[place.z] = kvsend[place.z]

    squares = ssa[place.z]
    for k in range(1, NZ):
        slot = ssar.at[place.along(-k)]
        sent(slot, slot, sa_sem.at[0, k], sa_sem.at[1, k], twin).wait_recv()
        squares = squares + ssar[place.along(-k)]
    scale = lax.rsqrt(squares[:1] / D + EPSILON)
    for k in range(NZ):
        slot = kvrecv.at[place.along(-k)]
        wait = sent(slot, slot, kv_sem.at[0, k], kv_sem.at[1, k], twin).wait_recv
        if k:
            wait()
        else:
            pl.when(place.moved != 0)(wait)
    kvown[...] = (jnp.sum(kvrecv[...].astype(F32), axis=0) * scale).astype(BF16)

    kvall[place.h, place.l, place.c, place.z] = kvown[...]

    def kz_copy(k):
        return sent(
            kvown, kvall.at[place.h, place.l, place.c, place.z],
            kz_sem.at[0, k], kz_sem.at[1, k], place.id(z=place.along(k)),
        )

    def ky_copy(side, k, ref):
        return sent(ref, ref, ky_sem.at[0, side, k], ky_sem.at[1, side, k], (above, below)[side])

    def kr_copy(k, ref):
        return sent(ref, ref, kr_sem.at[0, k], kr_sem.at[1, k], (above, below)[k % 2])

    def kd_copy(n, ref):
        return sent(ref, ref, kd_sem.at[0, n], kd_sem.at[1, n], place.partner())

    for k in along_order():
        kz_copy(k).start()
    sources = ((place.h, place.l), (dh, dl), (uh, ul), (1 - place.h, place.l))
    near = (0, 1, 7, 2, 6, 3, 5, 4)

    def piece(n, k):
        h, l = sources[n]
        return kvall.at[h, l, place.c, place.along(-k)]

    for k in near:
        if k:
            sent(piece(0, k), piece(0, k), kz_sem.at[0, k], kz_sem.at[1, k], twin).wait_recv()
        for side in range(2):
            ky_copy(side, k, piece(0, k)).start()
    kd_copy(0, kvall.at[place.h, place.l, place.c]).start()
    qt = qsend[place.z].astype(F32)
    for k in range(1, NZ):
        slot = qrecv.at[place.along(-k)]
        sent(slot, slot, q_sem.at[0, k], q_sem.at[1, k], twin).wait_recv()
        qt = qt + qrecv[place.along(-k)].astype(F32)
    qt = (qt * scale).astype(BF16)
    for k in near:
        ky_copy(0, k, piece(1, k)).wait_recv()
        if k % 2 == 0:
            kr_copy(k, piece(1, k)).start()
        ky_copy(1, k, piece(2, k)).wait_recv()
        if k % 2 == 1:
            kr_copy(k, piece(2, k)).start()
    for n in (1, 2):
        kd_copy(n, kvall.at[sources[n][0], sources[n][1], place.c]).start()
    for k in near:
        kr_copy(k, piece(3, k)).wait_recv()
    kd_copy(3, kvall.at[sources[3][0], sources[3][1], place.c]).start()
    for e in exchange[5:8]:
        e.start()
    for n in range(4):
        slot = kvall.at[sources[n][0], sources[n][1], 1 - place.c]
        kd_copy(n, slot).wait_recv()

    qblock = 2 * place.z + place.l

    def keyval(kind, l, z):
        return jnp.concatenate((kvall[kind, l, 0, z], kvall[kind, l, 1, z]), axis=0)

    def score(z, largest):
        for l in range(2):
            b = 2 * z + l
            s = lhs_t(keyval(0, l, z), qt) * HD ** (-0.5)
            shape = (MODAL_BLOCK, MODAL_BLOCK)
            key_pos = b * MODAL_BLOCK + lax.broadcasted_iota(jnp.int32, shape, 0)
            query_pos = qblock * MODAL_BLOCK + lax.broadcasted_iota(jnp.int32, shape, 1)
            s = jnp.where(key_pos <= query_pos, s, -1e30)
            scores[b] = s
            largest = jnp.maximum(largest, jnp.max(s, axis=0, keepdims=True))
        return largest

    largest = lax.fori_loop(0, NZ, score, jnp.full((1, MODAL_BLOCK), -1e30, F32))

    def power(b, norm):
        p = jnp.exp(scores[b] - largest)
        scores[b] = p
        return norm + jnp.sum(p, axis=0, keepdims=True)

    norm = lax.fori_loop(0, 2 * NZ, power, jnp.zeros((1, MODAL_BLOCK), F32))
    inverse = 1.0 / norm

    def weigh(z, ctx):
        for l in range(2):
            p = (scores[2 * z + l] * inverse).astype(BF16)
            ctx = ctx + jnp.dot(keyval(1, l, z), p, preferred_element_type=F32)
        return ctx

    ctxs[place.z] = lax.fori_loop(
        0, NZ, weigh, jnp.zeros((HD, MODAL_BLOCK), F32)
    ).astype(BF16)

    def cx_copy(k, owner):
        return sent(
            ctxs.at[owner], ctxs.at[owner], cx_sem.at[0, k], cx_sem.at[1, k],
            place.id(z=place.along(k)),
        )

    for k in along_order():
        cx_copy(k, place.z).start()
    loads[2].wait()
    exchange[3].wait_recv()
    for k in near:
        j = place.along(-k)
        if k:
            cx_copy(k, j).wait_recv()
        tower = towers[2 * j + place.l]
        parta[own, j] = jnp.dot(wo[0, tower], ctxs[j], preferred_element_type=F32).astype(BF16)
        parta[oth, j] = jnp.dot(wo[1, tower], ctxs[j], preferred_element_type=F32).astype(BF16)
    resid[...] = tokens[...].astype(F32) + reduce_rows(place, parta, dbufa, rbufa, ra_sem)

    src[...] = resid[...].astype(BF16)
    gather_rows(place, src, xg, g_sem)
    for load in loads[3:5]:
        load.wait()
    for e in exchange[4:8]:
        e.wait_recv()
    for e in exchange[8:]:
        e.start()

    def squares_to(k):
        j = place.along(k)
        return sent(ssp.at[j], ssr.at[place.z], s_sem.at[0, k], s_sem.at[1, k], place.id(z=j))

    def partial(j):
        tower = towers[2 * j + place.l]
        x0 = xg[own, j].astype(F32)
        x1 = xg[oth, j].astype(F32)
        ssp[j] = squares_of(x0, x1)
        n0 = (x0 * gcol[1, 0, tower]).astype(BF16)
        n1 = (x1 * gcol[1, 1, tower]).astype(BF16)
        for side, w in enumerate((wg, wu)):
            pbuf[j, side] = (lhs_t(n0, w[0, tower]) + lhs_t(n1, w[1, tower])).astype(BF16)

    sum_along_z(place, partial, pbuf, chain, c_sem)
    for k in range(1, NZ):
        squares_to(k).start()
    both = pbuf[place.z].astype(F32) + chain[0, 0].astype(F32) + chain[1, 0].astype(F32)
    squares = ssp[place.z]
    for k in range(1, NZ):
        slot = ssr.at[place.along(-k)]
        sent(slot, slot, s_sem.at[0, k], s_sem.at[1, k], twin).wait_recv()
        squares = squares + ssr[place.along(-k)]
    scale = as_column(lax.rsqrt(squares[:1] / D + EPSILON))
    gate = both[0] * scale
    up = both[1] * scale
    acts[place.z] = (gate / (1.0 + jnp.exp(-gate)) * up).astype(BF16)
    loads[5].wait()
    for e in exchange[8:]:
        e.wait_recv()

    def downward(j):
        tower = towers[2 * j + place.l]
        act = acts[j]
        part[own, j] = rhs_t(wd[0, tower], act).astype(BF16)
        part[oth, j] = rhs_t(wd[1, tower], act).astype(BF16)

    spread_along_z(place, acts, a_sem, downward)
    total = reduce_rows(place, part, dbuf, rbuf, r_sem)
    out[...] = (resid[...] + total).astype(BF16)

    gather_rows_end(place, tokens, xa, ga_sem)
    gather_rows_end(place, src, xg, g_sem)
    for e in exchange:
        e.wait_send()
    for k in range(1, NZ):
        squares_to(k).wait_send()
        q_copy(k).wait_send()
        kv_copy(k).wait_send()
        ssa_copy(k).wait_send()
        kz_copy(k).wait_send()
        cx_copy(k, place.z).wait_send()
    pl.when(place.moved != 0)(kv_copy(0).wait_send)
    for k in range(NZ):
        for side in range(2):
            ky_copy(side, k, piece(0, k)).wait_send()
        kr_copy(k, piece(1 + k % 2, k)).wait_send()
    for n in range(4):
        kd_copy(n, kvall.at[sources[n][0], sources[n][1], place.c]).wait_send()


def local(tokens, modality, attn_gain, ffn_gain, w_query, w_keyval, w_out, w_gate, w_up, w_down):
    feats = tokens.shape[1]
    width = w_gate.shape[2]
    kvw = w_keyval.shape[2]
    towers = modality.reshape(-1, MODAL_BLOCK)[:, 0]
    gains = jnp.concatenate((attn_gain, ffn_gain), axis=0)[:, None, :]
    vmem = pl.BlockSpec(memory_space=pltpu.VMEM)
    hbm = pl.BlockSpec(memory_space=pltpu.HBM)
    smem = pl.BlockSpec(memory_space=pltpu.SMEM)
    dma = pltpu.SemaphoreType.DMA
    rows = (feats, MODAL_BLOCK)
    result = pl.pallas_call(
        layer_kernel,
        out_shape=jax.ShapeDtypeStruct(rows, BF16),
        in_specs=[smem, vmem, vmem] + [hbm] * 6,
        out_specs=vmem,
        scratch_shapes=[
            pltpu.VMEM((2, NB, *rows), BF16),
            pltpu.VMEM((4, 1, feats), F32),
            pltpu.VMEM((2, 2, 2, *rows), F32),
            pltpu.VMEM((2, 2, feats, HD), BF16),
            pltpu.VMEM((2, 2, kvw, feats), BF16),
            pltpu.VMEM((2, 2, feats, HD), BF16),
            pltpu.VMEM((2, 2, feats, width), BF16),
            pltpu.VMEM((2, 2, feats, width), BF16),
            pltpu.VMEM((2, 2, feats, width), BF16),
            pltpu.VMEM((NZ, HD, MODAL_BLOCK), BF16),
            pltpu.VMEM((NZ, kvw, MODAL_BLOCK), BF16),
            pltpu.VMEM((NZ, HD, MODAL_BLOCK), BF16),
            pltpu.VMEM((NZ, kvw, MODAL_BLOCK), BF16),
            pltpu.VMEM((NZ, 8, MODAL_BLOCK), F32),
            pltpu.VMEM((NZ, 8, MODAL_BLOCK), F32),
            pltpu.VMEM((kvw, MODAL_BLOCK), BF16),
            pltpu.VMEM((2, 2, 2, NZ, kvw, MODAL_BLOCK), BF16),
            pltpu.VMEM((2 * NZ, MODAL_BLOCK, MODAL_BLOCK), F32),
            pltpu.VMEM((NZ, HD, MODAL_BLOCK), BF16),
            pltpu.VMEM((2, NB, *rows), BF16),
            pltpu.VMEM((NB, *rows), BF16),
            pltpu.VMEM((NB, *rows), BF16),
            pltpu.VMEM(rows, F32),
            pltpu.VMEM(rows, BF16),
            pltpu.VMEM((2, NB, *rows), BF16),
            pltpu.VMEM((NZ, 2, MODAL_BLOCK, width), BF16),
            pltpu.VMEM((2, 4, 2, MODAL_BLOCK, width), BF16),
            pltpu.VMEM((NZ, 8, MODAL_BLOCK), F32),
            pltpu.VMEM((NZ, 8, MODAL_BLOCK), F32),
            pltpu.VMEM((NZ, MODAL_BLOCK, width), BF16),
            pltpu.VMEM((2, NB, *rows), BF16),
            pltpu.VMEM((NB, *rows), BF16),
            pltpu.VMEM((NB, *rows), BF16),
            dma((6,)),
            dma((2, 10)),
            dma((4, NB)),
            dma((2, NZ)),
            dma((2, NZ)),
            dma((2, NZ)),
            dma((2, NZ)),
            dma((2, 2, NZ)),
            dma((2, NZ)),
            dma((2, 4)),
            dma((2, NZ)),
            dma((4, NB)),
            dma((4, NB)),
            dma((2, 2, 4, PARTS)),
            dma((2, NZ)),
            dma((2, 2, 4, 2)),
            dma((4, NB)),
        ],
        compiler_params=pltpu.CompilerParams(collective_id=0, has_side_effects=True),
        name="layer",
    )(
        towers,
        tokens.T,
        gains,
        w_query,
        jnp.swapaxes(w_keyval, 1, 2),
        jnp.swapaxes(w_out, 1, 2),
        w_gate,
        w_up,
        jnp.swapaxes(w_down, 1, 2),
    )
    return result.T


def solution(mesh):
    torus = Mesh(mesh.devices.reshape(NX, NYH, 2, 2, NZ), AXES)
    in_specs = (
        P(ROWS, MP),
        P(),
        P(None, MP),
        P(None, MP),
        P(None, MP, ROWS),
        P(None, MP, ROWS),
        P(None, ROWS, MP),
        P(None, MP, ROWS),
        P(None, MP, ROWS),
        P(None, ROWS, MP),
    )
    out_specs = P(ROWS, MP)
    return jax.shard_map(local, mesh=torus, in_specs=in_specs, out_specs=out_specs, check_vma=False)
```

time: 277 us -> 150 us (0.54)
  waiting for transfers between devices: 94.9 us -> 0 us
  Pallas kernels: 78.1 us -> 144 us
  blocking collectives: 43.8 us -> 0 us
  starting transfers between devices: 36.7 us -> 0 us
  local copies, waits for them, and re-layouts: 13.8 us -> 3.43 us
  other arithmetic: 4.16 us -> 0.01 us
    pallas_call x1, Pallas kernels: 78.1 us -> 144 us  [local(): pl.pallas_call(layer_kernel, out_shape=jax.ShapeDtypeStruct(rows, BF16),...]
    all_to_all x5 -> x0, waiting for transfers between devices: 55.3 us -> none  [the longest x4 55.3 us: from_everyone(): return lax.all_to_all(copies, axis, split_axis=0, concat_axis=0, tiled=True)]
    all_to_all x2 -> x0, blocking collectives: 43.8 us -> none  [the longest x1 24 us: sent_and_summed(): lax.all_to_all(blocks, axis, split_axis=0, concat_axis=0, tiled=True)]
    ppermute x4 -> x0, waiting for transfers between devices: 39.6 us -> none  [other(): return lax.ppermute(value, 'yl', [(0, 1), (1, 0)])]
    all_to_all x5 -> x0, starting transfers between devices: 32.7 us -> none  [the longest x4 27 us: from_everyone(): return lax.all_to_all(copies, axis, split_axis=0, concat_axis=0, tiled=True)]
    ppermute x4 -> x0, starting transfers between devices: 4.05 us -> none  [other(): return lax.ppermute(value, 'yl', [(0, 1), (1, 0)])]
    broadcast_in_dim x6 -> x1, local copies, waits for them, and re-layouts: 3.59 us -> 0.6 us  [local(): gains = jnp.concatenate((attn_gain, ffn_gain), axis=0)[:, None, :]]
  transfers between devices with their start and end apart: 9 -> 0, of which waited for: 6 -> 0; matrix products, arithmetic and copies ran while one was open for 3% -> 0% of each run, Pallas kernels for 0% -> 0%
where the time goes in v2:
time: 150 us; the launch traced here: 147 us
  Pallas kernels  144 us (96%)
  local copies, waits for them, and re-layouts  3.43 us (2%)
    pallas_call x1, Pallas kernels, local(): pl.pallas_call(layer_kernel, out_shape=jax.ShapeDtypeStruct(rows, BF16),...  144 us

profile of v2, /device:TPU:4, one launch (start us, length us, event | category | flops | bytes accessed | tf_op | source)
XLA Modules:
  0.0 147.4 jit_solution(6916825853326593651)
XLA Ops:
  0.0 0.0 copy-start
  0.0 0.7 copy-done
  0.7 0.0 copy-start.1
  0.7 0.0 copy-start.2
  0.7 0.6 slice_reduce_fusion.towers
  1.3 0.0 copy-done.1
  1.4 0.0 copy-done.2
  1.4 0.6 broadcast_in_dim.3.gains
  2.0 143.9 %layer.1 = bf16[224,128]{1,0:T(8,128)(2,1)} custom-call(s32[16]{0:T(128)} %slice_reduce_fusion.towers, bf16[224,128]{1,0:T(8,128)(2,1)} %bitcast.10, f32[4,1,224]{2,1,0:T(1,128)} %broadcast_in_dim.3.gains, bf16[2,224,128]{2,1,0:T(8,128)(2,1)} %wq_in.1, bf16[2,64,224]{2,1,0:T(8,128)(2,1)} %bitcast.9, bf16[2,224,128]{2,1,0:T(8,128)(2,1)} %bitcast.8, ...), custom_call_target="tpu_custom_call" | custom-call | tf_op jit(solution)/shard_map/layer/pallas_call | solution.py:603
  145.9 1.4 copy.12
  (1 shorter events, 0.0 us)
Async XLA Ops:
  0.0 0.7 copy-start
  0.7 0.7 copy-start.1
  0.7 0.7 copy-start.2

commit v3 on v2

--- a/solution.py
+++ b/solution.py
@@ -94,94 +94,123 @@
     pl.semaphore_wait(barrier, count + place.crossed + place.moved)
 
 
-def gather_rows(place, src, xg, sems):
-    send, recv, fsend, frecv = (sems.at[k] for k in range(4))
-    own = NYH * place.x + place.h
-    for i, (dx, dh) in enumerate(OFFSETS):
-        copy = sent(src, xg.at[place.l, own], send.at[i], recv.at[i], place.cross(dx, dh))
-        if (dx, dh) != (0, 0):
-            copy.start()
-        else:
-            pl.when(place.c != place.l)(copy.start)
-
-            @pl.when(place.c == place.l)
-            def _():
-                xg[place.l, own] = src[...]
-
-    order = sorted(range(NB), key=lambda i: (min(OFFSETS[i][0], NX - OFFSETS[i][0]), OFFSETS[i][1]))
-    for i in order:
-        dx, dh = OFFSETS[i]
-        slot = xg.at[place.c, place.behind(dx, dh)]
-        arrive = sent(slot, slot, send.at[i], recv.at[i], place.cross(dx, dh))
-        if (dx, dh) != (0, 0):
-            arrive.wait_recv()
-        else:
-            pl.when(place.c != place.l)(arrive.wait_recv)
-        sent(slot, slot, fsend.at[i], frecv.at[i], place.partner()).start()
-    for i in order:
-        dx, dh = OFFSETS[i]
-        slot = xg.at[1 - place.c, place.behind(dx, dh)]
-        sent(slot, slot, fsend.at[i], frecv.at[i], place.partner()).wait_recv()
-
-
-def gather_rows_end(place, src, xg, sems):
-    send, recv, fsend, frecv = (sems.at[k] for k in range(4))
-    for i, (dx, dh) in enumerate(OFFSETS):
-        copy = sent(src, src, send.at[i], recv.at[i], place.cross(dx, dh))
-        if (dx, dh) != (0, 0):
-            copy.wait_send()
-        else:
-            pl.when(place.c != place.l)(copy.wait_send)
-        slot = xg.at[place.c, place.behind(dx, dh)]
-        sent(slot, slot, fsend.at[i], frecv.at[i], place.partner()).wait_send()
-
-
-def reduce_rows(place, part, dbuf, rbuf, sems):
-    send, recv, fsend, frecv = (sems.at[k] for k in range(4))
-    own = NYH * place.x + place.h
-    for i, (dx, dh) in enumerate(OFFSETS):
-        j = place.ahead(dx, dh)
-        sent(
-            part.at[1 - place.c, j], dbuf.at[j], fsend.at[i], frecv.at[i], place.partner()
-        ).start()
-    for i, (dx, dh) in enumerate(OFFSETS):
-        j = place.ahead(dx, dh)
-        sent(part.at[1 - place.c, j], dbuf.at[j], fsend.at[i], frecv.at[i], place.partner()).wait_recv()
-        total = part[place.c, j].astype(F32) + dbuf[j].astype(F32)
-        dbuf[j] = total.astype(BF16)
-        copy = sent(dbuf.at[j], rbuf.at[i], send.at[i], recv.at[i], place.cross(dx, dh))
-        if (dx, dh) != (0, 0):
-            copy.start()
-        else:
-            pl.when(place.c != place.l)(copy.start)
-
-            @pl.when(place.c == place.l)
-            def _():
-                rbuf[i] = dbuf[own]
-
-    total = None
-    order = sorted(range(NB), key=lambda i: (min(OFFSETS[i][0], NX - OFFSETS[i][0]), OFFSETS[i][1]))
-    for i in order:
-        dx, dh = OFFSETS[i]
-        arrive = sent(rbuf.at[i], rbuf.at[i], send.at[i], recv.at[i], place.cross(dx, dh))
-        if (dx, dh) != (0, 0):
-            arrive.wait_recv()
-        else:
-            pl.when(place.c != place.l)(arrive.wait_recv)
-        term = rbuf[i].astype(F32)
-        total = term if total is None else total + term
-    for i, (dx, dh) in enumerate(OFFSETS):
-        j = place.ahead(dx, dh)
-        sent(part.at[1 - place.c, j], dbuf.at[j], fsend.at[i], frecv.at[i], place.partner()).wait_send()
-        copy = sent(dbuf.at[j], rbuf.at[i], send.at[i], recv.at[i], place.cross(dx, dh))
-        if (dx, dh) != (0, 0):
-            copy.wait_send()
-        else:
-            pl.when(place.c != place.l)(copy.wait_send)
-    return total
+def arrivals(place):
+    order = sorted(OFFSETS, key=lambda o: (min(o[0], NX - o[0]), o[1]))
+    return [place.behind(*o) for o in order]
+
+
+class RowGather:
+    def __init__(self, place, src, xg, sems):
+        self.place, self.src, self.xg = place, src, xg
+        self.send, self.recv, self.fsend, self.frecv = (sems.at[k] for k in range(4))
+        self.own = NYH * place.x + place.h
+
+    def away(self, j):
+        return jnp.logical_or(j != self.own, self.place.c != self.place.l)
+
+    def copy(self, i):
+        return sent(
+            self.src,
+            self.xg.at[self.place.l, self.own],
+            self.send.at[i],
+            self.recv.at[self.own],
+            self.place.cross(*OFFSETS[i]),
+        )
+
+    def start(self):
+        place = self.place
+        for i, offset in enumerate(OFFSETS):
+            if offset != (0, 0):
+                self.copy(i).start()
+            else:
+                pl.when(place.c != place.l)(self.copy(i).start)
+
+                @pl.when(place.c == place.l)
+                def _():
+                    self.xg[place.l, self.own] = self.src[...]
+
+    def forwarding(self, j, piece):
+        slot = self.xg.at[piece, j]
+        return sent(slot, slot, self.fsend.at[j], self.frecv.at[j], self.place.partner())
+
+    def forward(self, j):
+        slot = self.xg.at[self.place.c, j]
+        arrive = sent(slot, slot, self.send.at[0], self.recv.at[j], self.place.partner())
+        pl.when(self.away(j))(arrive.wait_recv)
+        self.forwarding(j, self.place.c).start()
+
+    def ready(self, j):
+        self.forwarding(j, 1 - self.place.c).wait_recv()
+
+    def end(self):
+        for i, offset in enumerate(OFFSETS):
+            if offset != (0, 0):
+                self.copy(i).wait_send()
+            else:
+                pl.when(self.place.c != self.place.l)(self.copy(i).wait_send)
+        for j in range(NB):
+            self.forwarding(j, self.place.c).wait_send()
+
+
+class RowSum:
+    def __init__(self, place, part, dbuf, rbuf, sems):
+        self.place, self.part, self.dbuf, self.rbuf = place, part, dbuf, rbuf
+        self.send, self.recv, self.fsend, self.frecv = (sems.at[k] for k in range(4))
+        self.own = NYH * place.x + place.h
+
+    def away(self, j):
+        return jnp.logical_or(j != self.own, self.place.c != self.place.l)
+
+    def pairing(self, j):
+        return sent(
+            self.part.at[1 - self.place.c, j],
+            self.dbuf.at[j],
+            self.fsend.at[j],
+            self.frecv.at[j],
+            self.place.partner(),
+        )
+
+    def copy(self, j):
+        return sent(
+            self.dbuf.at[j],
+            self.rbuf.at[self.own],
+            self.send.at[j],
+            self.recv.at[self.own],
+            self.place.id(x=j // NYH, yh=lax.rem(j, NYH), c=self.place.l, yl=self.place.c),
+        )
+
+    def pair(self, j):
+        self.pairing(j).start()
+
+    def pass_on(self, j):
+        self.pairing(j).wait_recv()
+        total = self.part[self.place.c, j].astype(F32) + self.dbuf[j].astype(F32)
+        self.dbuf[j] = total.astype(BF16)
+        pl.when(self.away(j))(self.copy(j).start)
+
+        @pl.when(jnp.logical_not(self.away(j)))
+        def _():
+            self.rbuf[self.own] = self.dbuf[self.own]
+
+    def finish(self):
+        total = None
+        for j in arrivals(self.place):
+            slot = self.rbuf.at[j]
+            arrive = sent(slot, slot, self.send.at[0], self.recv.at[j], self.place.partner())
+            pl.when(self.away(j))(arrive.wait_recv)
+            term = self.rbuf[j].astype(F32)
+            total = term if total is None else total + term
+        return total
+
+    def end(self):
+        for j in range(NB):
+            self.pairing(j).wait_send()
+            pl.when(self.away(j))(self.copy(j).wait_send)
 
 
 PARTS = 4
+LOOK = 3
+LAG = 2
 
 
 def sum_along_z(place, partial, pbuf, chain, sems):
@@ -240,25 +269,25 @@
 
 
 def spread_along_z(place, blocks, sems, on_arrival):
-    half = MODAL_BLOCK // 2
+    part_rows = MODAL_BLOCK // PARTS
     sides = (1, -1)
 
     def link(side, k, q, owner):
-        rows = blocks.at[owner, pl.ds(q * half, half), :]
+        rows = blocks.at[owner, pl.ds(q * part_rows, part_rows), :]
         return sent(
             rows, rows, sems.at[0, side, k - 1, q], sems.at[1, side, k - 1, q],
             place.id(z=place.along(sides[side])),
         )
 
     def used(side, k, q):
-        return k < 4 or q == side
-
-    for q in range(2):
+        return k < 4 or (q < PARTS // 2) == (side == 0)
+
+    for q in range(PARTS):
         for side in range(2):
             link(side, 1, q, place.z).start()
     on_arrival(place.z)
     for k in (1, 2, 3, 4):
-        for q in range(2):
+        for q in range(PARTS):
             for side in range(2):
                 if used(side, k, q):
                     owner = place.along(-k * sides[side])
@@ -271,7 +300,7 @@
         else:
             on_arrival(place.along(4))
     for k in (1, 2, 3, 4):
-        for q in range(2):
+        for q in range(PARTS):
             for side in range(2):
                 if used(side, k, q):
                     link(side, k, q, place.along(-(k - 1) * sides[side])).wait_send()
@@ -294,9 +323,9 @@
 
 
 def layer_kernel(
-    towers, tokens, gains, wq_in, wkv_in, wo_in, wg_in, wu_in, wd_in,
+    modality, tokens, again, fgain, wq_in, wkv_in, wo_in, wg_in, wu_in, wd_in,
     out,
-    xa, gother, gcol, wq, wkv, wo, wg, wu, wd,
+    xa, gother, fother, gcol, wq, wkv, wo, wg, wu, wd,
     qsend, kvsend, qrecv, kvrecv, ssa, ssar, kvown, kvall, scores, ctxs,
     parta, dbufa, rbufa, resid, src,
     xg, pbuf, chain, ssp, ssr, acts, part, dbuf, rbuf,
@@ -328,49 +357,75 @@
 
     exchange = []
     for k, (a, b) in enumerate(
-        [(gains, gother), (wq_in, wq.at[1]), (wkv_in, wkv.at[1]), (wo_in, wo.at[1])]
+        [(again, gother), (wq_in, wq.at[1]), (wkv_in, wkv.at[1]), (wo_in, wo.at[1])]
         + [(w.at[t], v.at[1, t]) for w, v in ((wg_in, wg), (wu_in, wu), (wd_in, wd)) for t in range(2)]
+        + [(fgain, fother)]
     ):
         exchange.append(sent(a, b, wsem.at[0, k], wsem.at[1, k], twin))
 
-    for e in exchange[:3]:
+    rows_in = RowGather(place, tokens, xa, ga_sem)
+    for e in exchange[:3] + exchange[10:]:
         e.start()
-    gather_rows(place, tokens, xa, ga_sem)
-    exchange[3].start()
-    exchange[4].start()
-
-    for e in exchange[:3]:
-        e.wait_recv()
+    rows_in.start()
+
+    def tower_of(j):
+        return modality[MODAL_BLOCK * (2 * j + place.l)]
+
+    exchange[0].wait_recv()
+    exchange[10].wait_recv()
     for t in range(2):
-        for which in range(2):
-            for piece, g in enumerate((gains, gother)):
-                row = jnp.broadcast_to(g[which * 2 + t], (MODAL_BLOCK, g.shape[2]))
+        for which, pair in enumerate(((again, gother), (fgain, fother))):
+            for piece, g in enumerate(pair):
+                row = jnp.broadcast_to(g[t : t + 1, :], (MODAL_BLOCK, g.shape[1]))
                 gcol[which, piece, t] = jnp.transpose(row)
     for load in loads[:2]:
         load.wait()
-
-    def q_copy(k):
-        j = place.along(k)
-        return sent(qsend.at[j], qrecv.at[place.z], q_sem.at[0, k], q_sem.at[1, k], place.id(z=j))
-
-    def kv_copy(k):
-        j = place.along(k)
-        return sent(
-            kvsend.at[j], kvrecv.at[place.z], kv_sem.at[0, k], kv_sem.at[1, k],
+    coming = arrivals(place)
+    for e in exchange[1:3]:
+        e.wait_recv()
+    for j in coming[:LOOK]:
+        rows_in.forward(j)
+
+    def q_copy(j):
+        return sent(
+            qsend.at[j], qrecv.at[place.z], q_sem.at[0, j], q_sem.at[1, place.z], place.id(z=j)
+        )
+
+    def kv_copy(j):
+        return sent(
+            kvsend.at[j], kvrecv.at[place.z], kv_sem.at[0, j], kv_sem.at[1, place.z],
             place.id(x=xd, yh=hd, z=j),
         )
 
-    def ssa_copy(k):
-        j = place.along(k)
-        return sent(ssa.at[j], ssar.at[place.z], sa_sem.at[0, k], sa_sem.at[1, k], place.id(z=j))
+    def ssa_copy(j):
+        return sent(
+            ssa.at[j], ssar.at[place.z], sa_sem.at[0, j], sa_sem.at[1, place.z], place.id(z=j)
+        )
+
+    def stays(j):
+        return jnp.logical_and(j == place.z, place.moved == 0)
+
+    def send_block(j):
+        pl.when(jnp.logical_not(stays(j)))(lambda: kv_copy(j).start())
+
+        @pl.when(stays(j))
+        def _():
+            kvrecv[place.z] = kvsend[place.z]
+
+        @pl.when(j != place.z)
+        def _():
+            q_copy(j).start()
+            ssa_copy(j).start()
 
     def squares_of(x0, x1):
         row = jnp.sum(x0 * x0, axis=0, keepdims=True) + jnp.sum(x1 * x1, axis=0, keepdims=True)
         return jnp.broadcast_to(row, (8, MODAL_BLOCK))
 
-    for k in along_order() + (0,):
-        j = place.along(k)
-        tower = towers[2 * j + place.l]
+    for n, j in enumerate(coming):
+        if n + LOOK < NB:
+            rows_in.forward(coming[n + LOOK])
+        rows_in.ready(j)
+        tower = tower_of(j)
         x0 = xa[own, j].astype(F32)
         x1 = xa[oth, j].astype(F32)
         ssa[j] = squares_of(x0, x1)
@@ -381,26 +436,19 @@
             jnp.dot(wkv[0, tower], n0, preferred_element_type=F32)
             + jnp.dot(wkv[1, tower], n1, preferred_element_type=F32)
         ).astype(BF16)
-        if k:
-            kv_copy(k).start()
-            q_copy(k).start()
-            ssa_copy(k).start()
-        else:
-            pl.when(place.moved != 0)(kv_copy(0).start)
-
-            @pl.when(place.moved == 0)
-            def _():
-                kvrecv[place.z] = kvsend[place.z]
-
+        send_block(j)
+
+    for e in exchange[3:6]:
+        e.start()
     squares = ssa[place.z]
     for k in range(1, NZ):
         slot = ssar.at[place.along(-k)]
-        sent(slot, slot, sa_sem.at[0, k], sa_sem.at[1, k], twin).wait_recv()
+        sent(slot, slot, sa_sem.at[0, k], sa_sem.at[1, place.along(-k)], twin).wait_recv()
         squares = squares + ssar[place.along(-k)]
     scale = lax.rsqrt(squares[:1] / D + EPSILON)
     for k in range(NZ):
         slot = kvrecv.at[place.along(-k)]
-        wait = sent(slot, slot, kv_sem.at[0, k], kv_sem.at[1, k], twin).wait_recv
+        wait = sent(slot, slot, kv_sem.at[0, k], kv_sem.at[1, place.along(-k)], twin).wait_recv
         if k:
             wait()
         else:
@@ -442,7 +490,7 @@
     qt = qsend[place.z].astype(F32)
     for k in range(1, NZ):
         slot = qrecv.at[place.along(-k)]
-        sent(slot, slot, q_sem.at[0, k], q_sem.at[1, k], twin).wait_recv()
+        sent(slot, slot, q_sem.at[0, k], q_sem.at[1, place.along(-k)], twin).wait_recv()
         qt = qt + qrecv[place.along(-k)].astype(F32)
     qt = (qt * scale).astype(BF16)
     for k in near:
@@ -457,7 +505,7 @@
     for k in near:
         kr_copy(k, piece(3, k)).wait_recv()
     kd_copy(3, kvall.at[sources[3][0], sources[3][1], place.c]).start()
-    for e in exchange[5:8]:
+    for e in exchange[6:8]:
         e.start()
     for n in range(4):
         slot = kvall.at[sources[n][0], sources[n][1], 1 - place.c]
@@ -500,40 +548,70 @@
         0, NZ, weigh, jnp.zeros((HD, MODAL_BLOCK), F32)
     ).astype(BF16)
 
-    def cx_copy(k, owner):
-        return sent(
-            ctxs.at[owner], ctxs.at[owner], cx_sem.at[0, k], cx_sem.at[1, k],
-            place.id(z=place.along(k)),
-        )
-
-    for k in along_order():
-        cx_copy(k, place.z).start()
+    def cx(k, owner):
+        first = 64 if k == -4 else 0
+        ref = ctxs.at[owner, pl.ds(first, HD // 2 if abs(k) == 4 else HD), :]
+        n = 0 if k == -4 else k % NZ
+        step = {3: 1, -3: -1, 4: 2, -4: -2}.get(k, k)
+        return sent(ref, ref, cx_sem.at[0, n], cx_sem.at[1, n], place.id(z=place.along(step)))
+
+    for k in (2, -2, 1, -1):
+        cx(k, place.z).start()
     loads[2].wait()
     exchange[3].wait_recv()
-    for k in near:
-        j = place.along(-k)
-        if k:
-            cx_copy(k, j).wait_recv()
-        tower = towers[2 * j + place.l]
+    rows_out = RowSum(place, parta, dbufa, rbufa, ra_sem)
+
+    def outward(j):
+        tower = tower_of(j)
         parta[own, j] = jnp.dot(wo[0, tower], ctxs[j], preferred_element_type=F32).astype(BF16)
         parta[oth, j] = jnp.dot(wo[1, tower], ctxs[j], preferred_element_type=F32).astype(BF16)
-    resid[...] = tokens[...].astype(F32) + reduce_rows(place, parta, dbufa, rbufa, ra_sem)
+        rows_out.pair(j)
+
+    outward(place.z)
+    for side in (1, -1):
+        owner = place.along(-2 * side)
+        cx(2 * side, owner).wait_recv()
+        cx(3 * side, owner).start()
+        cx(4 * side, owner).start()
+    last = place.z
+    for k in (1, -1, 2, -2, 3, -3, 4):
+        j = place.along(-k)
+        if abs(k) != 2:
+            cx(k, j).wait_recv()
+        if k == 4:
+            cx(-4, j).wait_recv()
+        outward(j)
+        rows_out.pass_on(last)
+        last = j
+    rows_out.pass_on(last)
+    resid[...] = tokens[...].astype(F32) + rows_out.finish()
 
     src[...] = resid[...].astype(BF16)
-    gather_rows(place, src, xg, g_sem)
+    rows_mid = RowGather(place, src, xg, g_sem)
+    rows_mid.start()
+    needed = [place.along(k) for k in (4, 3, -3, 2, -2, 1, -1, 0)]
+    for j in needed[:LOOK]:
+        rows_mid.forward(j)
     for load in loads[3:5]:
         load.wait()
     for e in exchange[4:8]:
         e.wait_recv()
-    for e in exchange[8:]:
+    for e in exchange[8:10]:
         e.start()
 
     def squares_to(k):
         j = place.along(k)
         return sent(ssp.at[j], ssr.at[place.z], s_sem.at[0, k], s_sem.at[1, k], place.id(z=j))
 
+    called = []
+
     def partial(j):
-        tower = towers[2 * j + place.l]
+        n = len(called)
+        called.append(j)
+        if n + LOOK < NB:
+            rows_mid.forward(needed[n + LOOK])
+        rows_mid.ready(needed[n])
+        tower = tower_of(j)
         x0 = xg[own, j].astype(F32)
         x1 = xg[oth, j].astype(F32)
         ssp[j] = squares_of(x0, x1)
@@ -541,10 +619,10 @@
         n1 = (x1 * gcol[1, 1, tower]).astype(BF16)
         for side, w in enumerate((wg, wu)):
             pbuf[j, side] = (lhs_t(n0, w[0, tower]) + lhs_t(n1, w[1, tower])).astype(BF16)
+        if n + 1 < NB:
+            squares_to((4, 3, -3, 2, -2, 1, -1)[n] % NZ).start()
 
     sum_along_z(place, partial, pbuf, chain, c_sem)
-    for k in range(1, NZ):
-        squares_to(k).start()
     both = pbuf[place.z].astype(F32) + chain[0, 0].astype(F32) + chain[1, 0].astype(F32)
     squares = ssp[place.z]
     for k in range(1, NZ):
@@ -556,31 +634,47 @@
     up = both[1] * scale
     acts[place.z] = (gate / (1.0 + jnp.exp(-gate)) * up).astype(BF16)
     loads[5].wait()
-    for e in exchange[8:]:
+    for e in exchange[8:10]:
         e.wait_recv()
 
+    rows_end = RowSum(place, part, dbuf, rbuf, r_sem)
+    done = []
+
     def downward(j):
-        tower = towers[2 * j + place.l]
+        tower = tower_of(j)
         act = acts[j]
         part[own, j] = rhs_t(wd[0, tower], act).astype(BF16)
         part[oth, j] = rhs_t(wd[1, tower], act).astype(BF16)
+        rows_end.pair(j)
+        if len(done) >= LAG:
+            rows_end.pass_on(done[-LAG])
+        done.append(j)
 
     spread_along_z(place, acts, a_sem, downward)
-    total = reduce_rows(place, part, dbuf, rbuf, r_sem)
+    for j in done[-LAG:]:
+        rows_end.pass_on(j)
+    total = rows_end.finish()
     out[...] = (resid[...] + total).astype(BF16)
 
-    gather_rows_end(place, tokens, xa, ga_sem)
-    gather_rows_end(place, src, xg, g_sem)
+    rows_in.end()
+    rows_mid.end()
+    rows_out.end()
+    rows_end.end()
     for e in exchange:
         e.wait_send()
     for k in range(1, NZ):
+        j = place.along(k)
         squares_to(k).wait_send()
-        q_copy(k).wait_send()
-        kv_copy(k).wait_send()
-        ssa_copy(k).wait_send()
+        q_copy(j).wait_send()
+        kv_copy(j).wait_send()
+        ssa_copy(j).wait_send()
         kz_copy(k).wait_send()
-        cx_copy(k, place.z).wait_send()
-    pl.when(place.moved != 0)(kv_copy(0).wait_send)
+    for side in (1, -1):
+        for k in (1, 2):
+            cx(k * side, place.z).wait_send()
+        for k in (3, 4):
+            cx(k * side, place.along(-2 * side)).wait_send()
+    pl.when(place.moved != 0)(kv_copy(place.z).wait_send)
     for k in range(NZ):
         for side in range(2):
             ky_copy(side, k, piece(0, k)).wait_send()
@@ -593,8 +687,6 @@
     feats = tokens.shape[1]
     width = w_gate.shape[2]
     kvw = w_keyval.shape[2]
-    towers = modality.reshape(-1, MODAL_BLOCK)[:, 0]
-    gains = jnp.concatenate((attn_gain, ffn_gain), axis=0)[:, None, :]
     vmem = pl.BlockSpec(memory_space=pltpu.VMEM)
     hbm = pl.BlockSpec(memory_space=pltpu.HBM)
     smem = pl.BlockSpec(memory_space=pltpu.SMEM)
@@ -603,11 +695,12 @@
     result = pl.pallas_call(
         layer_kernel,
         out_shape=jax.ShapeDtypeStruct(rows, BF16),
-        in_specs=[smem, vmem, vmem] + [hbm] * 6,
+        in_specs=[smem, vmem, vmem, vmem] + [hbm] * 6,
         out_specs=vmem,
         scratch_shapes=[
             pltpu.VMEM((2, NB, *rows), BF16),
-            pltpu.VMEM((4, 1, feats), F32),
+            pltpu.VMEM((2, feats), F32),
+            pltpu.VMEM((2, feats), F32),
             pltpu.VMEM((2, 2, 2, *rows), F32),
             pltpu.VMEM((2, 2, feats, HD), BF16),
             pltpu.VMEM((2, 2, kvw, feats), BF16),
@@ -640,7 +733,7 @@
             pltpu.VMEM((NB, *rows), BF16),
             pltpu.VMEM((NB, *rows), BF16),
             dma((6,)),
-            dma((2, 10)),
+            dma((2, 11)),
             dma((4, NB)),
             dma((2, NZ)),
             dma((2, NZ)),
@@ -654,15 +747,16 @@
             dma((4, NB)),
             dma((2, 2, 4, PARTS)),
             dma((2, NZ)),
-            dma((2, 2, 4, 2)),
+            dma((2, 2, 4, PARTS)),
             dma((4, NB)),
         ],
         compiler_params=pltpu.CompilerParams(collective_id=0, has_side_effects=True),
         name="layer",
     )(
-        towers,
+        modality,
         tokens.T,
-        gains,
+        attn_gain,
+        ffn_gain,
         w_query,
         jnp.swapaxes(w_keyval, 1, 2),
         jnp.swapaxes(w_out, 1, 2),

time: 150 us -> 140 us (0.933); the launches traced: 147 us -> 140 us
  Pallas kernels: 144 us -> 139 us
  local copies, waits for them, and re-layouts: 3.43 us -> 1.45 us
    pallas_call x1, Pallas kernels: 144 us -> 139 us  [local(): pl.pallas_call(layer_kernel, out_shape=jax.ShapeDtypeStruct(rows, BF16),...]
where the time goes in v3:
time: 140 us
  Pallas kernels  139 us (99%)
  local copies, waits for them, and re-layouts  1.45 us (1%)
    pallas_call x1, Pallas kernels, local(): pl.pallas_call(layer_kernel, out_shape=jax.ShapeDtypeStruct(rows, BF16),...  139 us

profile of v3, /device:TPU:4, one launch (start us, length us, event | category | flops | bytes accessed | tf_op | source)
XLA Modules:
  0.0 140.0 jit_solution(248537597418943640)
XLA Ops:
  0.0 138.6 %layer.1 = bf16[224,128]{1,0:T(8,128)(2,1)} custom-call(s32[2048]{0:T(1024)} %modality.1, bf16[224,128]{1,0:T(8,128)(2,1)} %bitcast.9, f32[2,224]{1,0:T(2,128)} %again.1, f32[2,224]{1,0:T(2,128)} %fgain.1, bf16[2,224,128]{2,1,0:T(8,128)(2,1)} %wq_in.1, bf16[2,64,224]{2,1,0:T(8,128)(2,1)} %bitcast.8, bf16[2,224,128]{2,1,0:T(8,128)(2,1)} %bitcast.7, ...), custom_call_target="tpu_custom_call" | custom-call | tf_op jit(solution)/shard_map/layer/pallas_call | solution.py:695
  138.6 1.4 %copy.12 = bf16[128,224]{0,1:T(8,128)(2,1)} copy(bf16[128,224]{0,1:T(8,128)(2,1)} %bitcast.6) | data formatting | bytes 114688

commit v4 on v3

--- a/solution.py
+++ b/solution.py
@@ -209,16 +209,23 @@
 
 
 PARTS = 4
+
+
+def part_of(width, q):
+    tiles = width // 16
+    starts = [16 * (tiles * p // PARTS) for p in range(PARTS)] + [width]
+    return pl.ds(starts[q], starts[q + 1] - starts[q])
+
+
 LOOK = 3
 LAG = 2
 
 
-def sum_along_z(place, partial, pbuf, chain, sems):
-    part_rows = MODAL_BLOCK // PARTS
+def sum_along_z(place, partial, pbuf, chain, sems, on_part):
     sides = (1, -1)
 
     def rows(q):
-        return pl.ds(q * part_rows, part_rows)
+        return part_of(pbuf.shape[2], q)
 
     def hops(side, q):
         long = (q < PARTS // 2) == (side == 0)
@@ -262,48 +269,54 @@
         for side in range(2):
             slot = chain.at[side, 0, :, rows(q), :]
             link(side, 1, q, slot).wait_recv()
+        on_part(q, rows(q))
     for q in range(PARTS):
         for side in range(2):
             for k in range(1, hops(side, q) + 1):
                 link(side, k, q, chain.at[side, k - 1, :, rows(q), :]).wait_send()
 
 
-def spread_along_z(place, blocks, sems, on_arrival):
-    part_rows = MODAL_BLOCK // PARTS
-    sides = (1, -1)
-
-    def link(side, k, q, owner):
-        rows = blocks.at[owner, pl.ds(q * part_rows, part_rows), :]
+class Ring:
+    def __init__(self, place, blocks, sems):
+        self.place, self.blocks, self.sems = place, blocks, sems
+        self.all = [(q, side) for q in range(PARTS) for side in range(2)]
+
+    def link(self, side, k, q, owner):
+        rows = self.blocks.at[owner, part_of(self.blocks.shape[1], q), :]
+        step = (1, -1)[side]
         return sent(
-            rows, rows, sems.at[0, side, k - 1, q], sems.at[1, side, k - 1, q],
-            place.id(z=place.along(sides[side])),
-        )
-
-    def used(side, k, q):
+            rows,
+            rows,
+            self.sems.at[0, side, k - 1, q],
+            self.sems.at[1, side, k - 1, q],
+            self.place.id(z=self.place.along(step)),
+        )
+
+    def used(self, side, k, q):
         return k < 4 or (q < PARTS // 2) == (side == 0)
 
-    for q in range(PARTS):
+    def start(self, q):
         for side in range(2):
-            link(side, 1, q, place.z).start()
-    on_arrival(place.z)
-    for k in (1, 2, 3, 4):
-        for q in range(PARTS):
-            for side in range(2):
-                if used(side, k, q):
-                    owner = place.along(-k * sides[side])
-                    link(side, k, q, owner).wait_recv()
-                    if k < 4 and used(side, k + 1, q):
-                        link(side, k + 1, q, owner).start()
-        if k < 4:
-            for side in range(2):
-                on_arrival(place.along(-k * sides[side]))
-        else:
-            on_arrival(place.along(4))
-    for k in (1, 2, 3, 4):
-        for q in range(PARTS):
-            for side in range(2):
-                if used(side, k, q):
-                    link(side, k, q, place.along(-(k - 1) * sides[side])).wait_send()
+            self.link(side, 1, q, self.place.z).start()
+
+    def run(self, on_arrival):
+        on_arrival(self.place.z)
+        for k in (1, 2, 3, 4):
+            for q, side in self.all:
+                if self.used(side, k, q):
+                    owner = self.place.along((-k, k)[side])
+                    self.link(side, k, q, owner).wait_recv()
+                    if k < 4 and self.used(side, k + 1, q):
+                        self.link(side, k + 1, q, owner).start()
+            on_arrival(self.place.along(-k))
+            if k < 4:
+                on_arrival(self.place.along(k))
+
+    def end(self):
+        for k in (1, 2, 3, 4):
+            for q, side in self.all:
+                if self.used(side, k, q):
+                    self.link(side, k, q, self.place.along((1 - k, k - 1)[side])).wait_send()
 
 
 def along_order():
@@ -316,17 +329,13 @@
 
 def rhs_t(a, b):
     return lax.dot_general(a, b, (((1,), (1,)), ((), ())), preferred_element_type=F32)
-
-
-def as_column(row):
-    return jnp.transpose(jnp.broadcast_to(row, (MODAL_BLOCK, MODAL_BLOCK)))[:, :1]
 
 
 def layer_kernel(
     modality, tokens, again, fgain, wq_in, wkv_in, wo_in, wg_in, wu_in, wd_in,
     out,
     xa, gother, fother, gcol, wq, wkv, wo, wg, wu, wd,
-    qsend, kvsend, qrecv, kvrecv, ssa, ssar, kvown, kvall, scores, ctxs,
+    turned, qsend, kvsend, qrecv, kvrecv, ssa, ssar, kvown, kvall, scores, ctxs,
     parta, dbufa, rbufa, resid, src,
     xg, pbuf, chain, ssp, ssr, acts, part, dbuf, rbuf,
     lsem, wsem, ga_sem, q_sem, kv_sem, sa_sem, kz_sem, ky_sem, kr_sem, kd_sem, cx_sem, ra_sem,
@@ -440,6 +449,15 @@
 
     for e in exchange[3:6]:
         e.start()
+    def turn(side, piece):
+        for t in range(2):
+            turned[side, piece, t] = jnp.transpose(
+                (wg, wu)[side][piece, t].astype(F32)
+            ).astype(BF16)
+
+    for side in range(2):
+        loads[3 + side].wait()
+        turn(side, 0)
     squares = ssa[place.z]
     for k in range(1, NZ):
         slot = ssar.at[place.along(-k)]
@@ -492,7 +510,8 @@
         slot = qrecv.at[place.along(-k)]
         sent(slot, slot, q_sem.at[0, k], q_sem.at[1, place.along(-k)], twin).wait_recv()
         qt = qt + qrecv[place.along(-k)].astype(F32)
-    qt = (qt * scale).astype(BF16)
+    qt = qt * scale
+    qt = qt.astype(BF16).astype(F32)
     for k in near:
         ky_copy(0, k, piece(1, k)).wait_recv()
         if k % 2 == 0:
@@ -516,37 +535,30 @@
     def keyval(kind, l, z):
         return jnp.concatenate((kvall[kind, l, 0, z], kvall[kind, l, 1, z]), axis=0)
 
-    def score(z, largest):
+    shape = (MODAL_BLOCK, MODAL_BLOCK)
+    query = jnp.transpose(qt).astype(BF16)
+    ahead = lax.broadcasted_iota(jnp.int32, shape, 1) - lax.broadcasted_iota(jnp.int32, shape, 0)
+    largest = jnp.full(shape, -1e30, F32)
+    for z in range(NZ):
         for l in range(2):
             b = 2 * z + l
-            s = lhs_t(keyval(0, l, z), qt) * HD ** (-0.5)
-            shape = (MODAL_BLOCK, MODAL_BLOCK)
-            key_pos = b * MODAL_BLOCK + lax.broadcasted_iota(jnp.int32, shape, 0)
-            query_pos = qblock * MODAL_BLOCK + lax.broadcasted_iota(jnp.int32, shape, 1)
-            s = jnp.where(key_pos <= query_pos, s, -1e30)
+            s = jnp.dot(query, keyval(0, l, z), preferred_element_type=F32) * HD ** (-0.5)
+            s = jnp.where(ahead <= (qblock - b) * MODAL_BLOCK, s, -1e30)
             scores[b] = s
-            largest = jnp.maximum(largest, jnp.max(s, axis=0, keepdims=True))
-        return largest
-
-    largest = lax.fori_loop(0, NZ, score, jnp.full((1, MODAL_BLOCK), -1e30, F32))
-
-    def power(b, norm):
+            largest = jnp.maximum(largest, s)
+    largest = jnp.max(largest, axis=1, keepdims=True)
+    norm = jnp.zeros(shape, F32)
+    for b in range(2 * NZ):
         p = jnp.exp(scores[b] - largest)
         scores[b] = p
-        return norm + jnp.sum(p, axis=0, keepdims=True)
-
-    norm = lax.fori_loop(0, 2 * NZ, power, jnp.zeros((1, MODAL_BLOCK), F32))
-    inverse = 1.0 / norm
-
-    def weigh(z, ctx):
+        norm = norm + p
+    inverse = 1.0 / jnp.sum(norm, axis=1, keepdims=True)
+    ctx = jnp.zeros((MODAL_BLOCK, HD), F32)
+    for z in range(NZ):
         for l in range(2):
             p = (scores[2 * z + l] * inverse).astype(BF16)
-            ctx = ctx + jnp.dot(keyval(1, l, z), p, preferred_element_type=F32)
-        return ctx
-
-    ctxs[place.z] = lax.fori_loop(
-        0, NZ, weigh, jnp.zeros((HD, MODAL_BLOCK), F32)
-    ).astype(BF16)
+            ctx = ctx + rhs_t(p, keyval(1, l, z))
+    ctxs[place.z] = jnp.transpose(ctx).astype(BF16)
 
     def cx(k, owner):
         first = 64 if k == -4 else 0
@@ -557,6 +569,9 @@
 
     for k in (2, -2, 1, -1):
         cx(k, place.z).start()
+    for e in exchange[4:6]:
+        e.wait_recv()
+    turn(0, 1)
     loads[2].wait()
     exchange[3].wait_recv()
     rows_out = RowSum(place, parta, dbufa, rbufa, ra_sem)
@@ -573,7 +588,7 @@
         cx(2 * side, owner).wait_recv()
         cx(3 * side, owner).start()
         cx(4 * side, owner).start()
-    last = place.z
+    sums = [place.z]
     for k in (1, -1, 2, -2, 3, -3, 4):
         j = place.along(-k)
         if abs(k) != 2:
@@ -581,21 +596,22 @@
         if k == 4:
             cx(-4, j).wait_recv()
         outward(j)
-        rows_out.pass_on(last)
-        last = j
-    rows_out.pass_on(last)
+        if len(sums) >= LAG:
+            rows_out.pass_on(sums[-LAG])
+        sums.append(j)
+    for j in sums[-LAG:]:
+        rows_out.pass_on(j)
     resid[...] = tokens[...].astype(F32) + rows_out.finish()
 
     src[...] = resid[...].astype(BF16)
     rows_mid = RowGather(place, src, xg, g_sem)
     rows_mid.start()
+    for e in exchange[6:8]:
+        e.wait_recv()
+    turn(1, 1)
     needed = [place.along(k) for k in (4, 3, -3, 2, -2, 1, -1, 0)]
     for j in needed[:LOOK]:
         rows_mid.forward(j)
-    for load in loads[3:5]:
-        load.wait()
-    for e in exchange[4:8]:
-        e.wait_recv()
     for e in exchange[8:10]:
         e.start()
 
@@ -617,45 +633,61 @@
         ssp[j] = squares_of(x0, x1)
         n0 = (x0 * gcol[1, 0, tower]).astype(BF16)
         n1 = (x1 * gcol[1, 1, tower]).astype(BF16)
-        for side, w in enumerate((wg, wu)):
-            pbuf[j, side] = (lhs_t(n0, w[0, tower]) + lhs_t(n1, w[1, tower])).astype(BF16)
+        for side in range(2):
+            pbuf[j, side] = (
+                jnp.dot(turned[side, 0, tower], n0, preferred_element_type=F32)
+                + jnp.dot(turned[side, 1, tower], n1, preferred_element_type=F32)
+            ).astype(BF16)
         if n + 1 < NB:
             squares_to((4, 3, -3, 2, -2, 1, -1)[n] % NZ).start()
 
-    sum_along_z(place, partial, pbuf, chain, c_sem)
-    both = pbuf[place.z].astype(F32) + chain[0, 0].astype(F32) + chain[1, 0].astype(F32)
-    squares = ssp[place.z]
-    for k in range(1, NZ):
-        slot = ssr.at[place.along(-k)]
-        sent(slot, slot, s_sem.at[0, k], s_sem.at[1, k], twin).wait_recv()
-        squares = squares + ssr[place.along(-k)]
-    scale = as_column(lax.rsqrt(squares[:1] / D + EPSILON))
-    gate = both[0] * scale
-    up = both[1] * scale
-    acts[place.z] = (gate / (1.0 + jnp.exp(-gate)) * up).astype(BF16)
+    ring = Ring(place, acts, a_sem)
+    scales = []
+
+    def activate(q, rows):
+        if not scales:
+            squares = ssp[place.z]
+            for k in range(1, NZ):
+                slot = ssr.at[place.along(-k)]
+                sent(slot, slot, s_sem.at[0, k], s_sem.at[1, k], twin).wait_recv()
+                squares = squares + ssr[place.along(-k)]
+            scales.append(lax.rsqrt(squares[:1] / D + EPSILON))
+        gate, up = (
+            (
+                pbuf[place.z, side, rows, :].astype(F32)
+                + chain[0, 0, side, rows, :].astype(F32)
+                + chain[1, 0, side, rows, :].astype(F32)
+            )
+            * scales[0]
+            for side in range(2)
+        )
+        acts[place.z, rows, :] = (gate / (1.0 + jnp.exp(-gate)) * up).astype(BF16)
+        ring.start(q)
+
+    sum_along_z(place, partial, pbuf, chain, c_sem, activate)
     loads[5].wait()
     for e in exchange[8:10]:
         e.wait_recv()
-
     rows_end = RowSum(place, part, dbuf, rbuf, r_sem)
     done = []
 
     def downward(j):
         tower = tower_of(j)
         act = acts[j]
-        part[own, j] = rhs_t(wd[0, tower], act).astype(BF16)
-        part[oth, j] = rhs_t(wd[1, tower], act).astype(BF16)
+        part[own, j] = jnp.dot(wd[0, tower], act, preferred_element_type=F32).astype(BF16)
+        part[oth, j] = jnp.dot(wd[1, tower], act, preferred_element_type=F32).astype(BF16)
         rows_end.pair(j)
         if len(done) >= LAG:
             rows_end.pass_on(done[-LAG])
         done.append(j)
 
-    spread_along_z(place, acts, a_sem, downward)
+    ring.run(downward)
     for j in done[-LAG:]:
         rows_end.pass_on(j)
     total = rows_end.finish()
     out[...] = (resid[...] + total).astype(BF16)
 
+    ring.end()
     rows_in.end()
     rows_mid.end()
     rows_out.end()
@@ -708,6 +740,7 @@
             pltpu.VMEM((2, 2, feats, width), BF16),
             pltpu.VMEM((2, 2, feats, width), BF16),
             pltpu.VMEM((2, 2, feats, width), BF16),
+            pltpu.VMEM((2, 2, 2, width, feats), BF16),
             pltpu.VMEM((NZ, HD, MODAL_BLOCK), BF16),
             pltpu.VMEM((NZ, kvw, MODAL_BLOCK), BF16),
             pltpu.VMEM((NZ, HD, MODAL_BLOCK), BF16),
@@ -724,11 +757,11 @@
             pltpu.VMEM(rows, F32),
             pltpu.VMEM(rows, BF16),
             pltpu.VMEM((2, NB, *rows), BF16),
-            pltpu.VMEM((NZ, 2, MODAL_BLOCK, width), BF16),
-            pltpu.VMEM((2, 4, 2, MODAL_BLOCK, width), BF16),
+            pltpu.VMEM((NZ, 2, width, MODAL_BLOCK), BF16),
+            pltpu.VMEM((2, 4, 2, width, MODAL_BLOCK), BF16),
             pltpu.VMEM((NZ, 8, MODAL_BLOCK), F32),
             pltpu.VMEM((NZ, 8, MODAL_BLOCK), F32),
-            pltpu.VMEM((NZ, MODAL_BLOCK, width), BF16),
+            pltpu.VMEM((NZ, width, MODAL_BLOCK), BF16),
             pltpu.VMEM((2, NB, *rows), BF16),
             pltpu.VMEM((NB, *rows), BF16),
             pltpu.VMEM((NB, *rows), BF16),

time: 140 us -> 132 us (0.943)
  Pallas kernels: 139 us -> 130 us
    pallas_call x1, Pallas kernels: 139 us -> 130 us  [local(): pl.pallas_call(layer_kernel, out_shape=jax.ShapeDtypeStruct(rows, BF16),...]
where the time goes in v4:
time: 132 us
  Pallas kernels  130 us (98%)
  local copies, waits for them, and re-layouts  1.45 us (1%)
    pallas_call x1, Pallas kernels, local(): pl.pallas_call(layer_kernel, out_shape=jax.ShapeDtypeStruct(rows, BF16),...  130 us

profile of v4, /device:TPU:4, one launch (start us, length us, event | category | flops | bytes accessed | tf_op | source)
XLA Modules:
  0.0 131.5 jit_solution(15902356426647914226)
XLA Ops:
  0.0 130.1 %layer.1 = bf16[224,128]{1,0:T(8,128)(2,1)} custom-call(s32[2048]{0:T(1024)} %modality.1, bf16[224,128]{1,0:T(8,128)(2,1)} %bitcast.9, f32[2,224]{1,0:T(2,128)} %again.1, f32[2,224]{1,0:T(2,128)} %fgain.1, bf16[2,224,128]{2,1,0:T(8,128)(2,1)} %wq_in.1, bf16[2,64,224]{2,1,0:T(8,128)(2,1)} %bitcast.8, bf16[2,224,128]{2,1,0:T(8,128)(2,1)} %bitcast.7, ...), custom_call_target="tpu_custom_call" | custom-call | tf_op jit(solution)/shard_map/layer/pallas_call | solution.py:727
  130.1 1.4 %copy.12 = bf16[128,224]{0,1:T(8,128)(2,1)} copy(bf16[128,224]{0,1:T(8,128)(2,1)} %bitcast.6) | data formatting | bytes 114688

commit v5 on v4

--- a/solution.py
+++ b/solution.py
@@ -208,7 +208,7 @@
             pl.when(self.away(j))(self.copy(j).wait_send)
 
 
-PARTS = 4
+PARTS = 8
 
 
 def part_of(width, q):
@@ -430,6 +430,8 @@
         row = jnp.sum(x0 * x0, axis=0, keepdims=True) + jnp.sum(x1 * x1, axis=0, keepdims=True)
         return jnp.broadcast_to(row, (8, MODAL_BLOCK))
 
+    for e in exchange[3:6]:
+        e.start()
     for n, j in enumerate(coming):
         if n + LOOK < NB:
             rows_in.forward(coming[n + LOOK])
@@ -447,8 +449,6 @@
         ).astype(BF16)
         send_block(j)
 
-    for e in exchange[3:6]:
-        e.start()
     def turn(side, piece):
         for t in range(2):
             turned[side, piece, t] = jnp.transpose(

time: 132 us -> 131 us (level)
  no operation moved by 1% of the time
where the time goes in v5:
time: 131 us
  Pallas kernels  130 us (99%)
  local copies, waits for them, and re-layouts  1.45 us (1%)
    pallas_call x1, Pallas kernels, local(): pl.pallas_call(layer_kernel, out_shape=jax.ShapeDtypeStruct(rows, BF16),...  130 us

profile of v5, /device:TPU:4, one launch (start us, length us, event | category | flops | bytes accessed | tf_op | source)
XLA Modules:
  0.0 131.1 jit_solution(250330468138754010)
XLA Ops:
  0.0 129.7 %layer.1 = bf16[224,128]{1,0:T(8,128)(2,1)} custom-call(s32[2048]{0:T(1024)} %modality.1, bf16[224,128]{1,0:T(8,128)(2,1)} %bitcast.9, f32[2,224]{1,0:T(2,128)} %again.1, f32[2,224]{1,0:T(2,128)} %fgain.1, bf16[2,224,128]{2,1,0:T(8,128)(2,1)} %wq_in.1, bf16[2,64,224]{2,1,0:T(8,128)(2,1)} %bitcast.8, bf16[2,224,128]{2,1,0:T(8,128)(2,1)} %bitcast.7, ...), custom_call_target="tpu_custom_call" | custom-call | tf_op jit(solution)/shard_map/layer/pallas_call | solution.py:727
  129.7 1.4 %copy.12 = bf16[128,224]{0,1:T(8,128)(2,1)} copy(bf16[128,224]{0,1:T(8,128)(2,1)} %bitcast.6) | data formatting | bytes 114688

commit v6 on v5

--- a/solution.py
+++ b/solution.py
@@ -61,7 +61,7 @@
         return NYH * self.h + self.x // NYH, lax.rem(self.x, NYH)
 
 
-OFFSETS = tuple((dx, dh) for dx in (2, 1, 3, 0) for dh in (1, 0))
+OFFSETS = tuple((dx, dh) for dx in (1, 3, 2, 0) for dh in (1, 0))
 
 
 def sent(src, dst, send, recv, target):
@@ -218,7 +218,7 @@
 
 
 LOOK = 3
-LAG = 2
+LAG = 3
 
 
 def sum_along_z(place, partial, pbuf, chain, sems, on_part):

time: 131 us -> 131 us (level)
  no operation moved by 1% of the time
where the time goes in v6:
time: 131 us
  Pallas kernels  130 us (99%)
  local copies, waits for them, and re-layouts  1.45 us (1%)
    pallas_call x1, Pallas kernels, local(): pl.pallas_call(layer_kernel, out_shape=jax.ShapeDtypeStruct(rows, BF16),...  130 us

profile of v6, /device:TPU:4, one launch (start us, length us, event | category | flops | bytes accessed | tf_op | source)
XLA Modules:
  0.0 131.4 jit_solution(7169726620050474490)
XLA Ops:
  0.0 130.0 %layer.1 = bf16[224,128]{1,0:T(8,128)(2,1)} custom-call(s32[2048]{0:T(1024)} %modality.1, bf16[224,128]{1,0:T(8,128)(2,1)} %bitcast.9, f32[2,224]{1,0:T(2,128)} %again.1, f32[2,224]{1,0:T(2,128)} %fgain.1, bf16[2,224,128]{2,1,0:T(8,128)(2,1)} %wq_in.1, bf16[2,64,224]{2,1,0:T(8,128)(2,1)} %bitcast.8, bf16[2,224,128]{2,1,0:T(8,128)(2,1)} %bitcast.7, ...), custom_call_target="tpu_custom_call" | custom-call | tf_op jit(solution)/shard_map/layer/pallas_call | solution.py:727
  130.0 1.4 %copy.12 = bf16[128,224]{0,1:T(8,128)(2,1)} copy(bf16[128,224]{0,1:T(8,128)(2,1)} %bitcast.6) | data formatting | bytes 114688
